TPU v7x, 16 devices: a whole 2x2x2 slice. The times are simulated.
16 devices in a mesh: dp: 4 (over z, y), sp: 4 (over x, core).
Axes of the slice: x: 2, y: 2, z: 2, core: 2. Of those that a mesh axis runs over, the one named last changes fastest.
Arguments:
- latents: bfloat16 [24, 8, 128, 1280], P('dp', 'sp'), parts along dimension 0
- time_emb: bfloat16 [24, 1280], P('dp'), parts along dimension 0
- context: bfloat16 [24, 77, 1024], P('dp'), parts along dimension 0
- res_norm: float32 [2, 2, 2, 1280], replicated
- res_conv_w: bfloat16 [2, 2, 3, 3, 1280, 1280], replicated
- res_conv_b: float32 [2, 2, 1280], replicated
- res_temb_w: bfloat16 [2, 1280, 1280], replicated
- res_temb_b: float32 [2, 1280], replicated
- tr_norm: float32 [2, 1280], replicated
- proj_w: bfloat16 [2, 1280, 1280], replicated
- proj_b: float32 [2, 1280], replicated
- ln_par: float32 [2, 3, 2, 1280], replicated
- self_qkv: bfloat16 [2, 3, 1280, 20, 64], replicated
- cross_q: bfloat16 [2, 1280, 20, 64], replicated
- cross_kv: bfloat16 [2, 2, 1024, 20, 64], replicated
- attn_out: bfloat16 [2, 2, 20, 64, 1280], replicated
- attn_b: float32 [2, 2, 1280], replicated
- ff_in_w: bfloat16 [2, 1280, 10240], replicated
- ff_in_b: float32 [2, 10240], replicated
- ff_out_w: bfloat16 [2, 5120, 1280], replicated
- ff_out_b: float32 [2, 1280], replicated
Outputs:
- output: bfloat16 [24, 8, 128, 1280], P('dp', 'sp'), parts along dimension 0
There are 4 independent parts. A program takes and returns all parts, laid end to end along the dimension named above; an argument that names none is the same for every part.
All inputs are finite; a program needn't handle non-finite values.
Results may differ from a plain program's by a relative error of at most 0.0194881.
Values are sent between devices in bfloat16 or wider.
A program may use at most 1.25 GiB of HBM per device.

v0:
```python
import functools
import math
import jax
import jax.numpy as jnp
from jax import lax
from jax.sharding import PartitionSpec as P

NUM_GROUPS = 32


def group_norm_sp(values, norm_gain, norm_bias, eps_val, sp_size):
    batch_n, rows_n, cols_n, chan_n = values.shape
    grouped = values.astype(jnp.float32).reshape(batch_n, rows_n, cols_n, NUM_GROUPS, chan_n // NUM_GROUPS)
    local_sums = jnp.stack([grouped.sum(axis=(1, 2, 4)), (grouped * grouped).sum(axis=(1, 2, 4))])
    total_sums = lax.psum(local_sums, 'sp')
    count_n = rows_n * sp_size * cols_n * (chan_n // NUM_GROUPS)
    grp_mean = total_sums[0] / count_n
    grp_var = total_sums[1] / count_n - grp_mean * grp_mean
    inv_std = lax.rsqrt(grp_var + eps_val)
    normed = (grouped - grp_mean[:, None, None, :, None]) * inv_std[:, None, None, :, None]
    return normed.reshape(batch_n, rows_n, cols_n, chan_n) * norm_gain + norm_bias


def conv_rows(act_in, kernel, sp_size):
    to_next = [(position, position + 1) for position in range(sp_size - 1)]
    to_prev = [(position + 1, position) for position in range(sp_size - 1)]
    from_above = lax.ppermute(act_in[:, -1:], 'sp', to_next)
    from_below = lax.ppermute(act_in[:, :1], 'sp', to_prev)
    padded = jnp.concatenate([from_above, act_in, from_below], axis=1)
    return lax.conv_general_dilated(padded, kernel, (1, 1), ((0, 0), (1, 1)), dimension_numbers=('NHWC', 'HWIO', 'NHWC'), preferred_element_type=jnp.float32)


def resnet_local(latents, time_emb, res_index, res_norm, res_conv_w, res_conv_b, res_temb_w, res_temb_b, sp_size):
    first_act = jax.nn.silu(group_norm_sp(latents, res_norm[res_index, 0, 0], res_norm[res_index, 0, 1], 1e-5, sp_size)).astype(jnp.bfloat16)
    time_proj = jnp.dot(jax.nn.silu(time_emb.astype(jnp.float32)).astype(jnp.bfloat16), res_temb_w[res_index], preferred_element_type=jnp.float32) + res_temb_b[res_index]
    hidden = (conv_rows(first_act, res_conv_w[res_index, 0], sp_size) + res_conv_b[res_index, 0] + time_proj[:, None, None, :]).astype(jnp.bfloat16)
    second_act = jax.nn.silu(group_norm_sp(hidden, res_norm[res_index, 1, 0], res_norm[res_index, 1, 1], 1e-5, sp_size)).astype(jnp.bfloat16)
    update = conv_rows(second_act, res_conv_w[res_index, 1], sp_size) + res_conv_b[res_index, 1]
    return (latents.astype(jnp.float32) + update).astype(jnp.bfloat16)


def layer_norm(values, norm_gain, norm_bias):
    centered = values.astype(jnp.float32)
    centered = centered - centered.mean(axis=-1, keepdims=True)
    variance = (centered * centered).mean(axis=-1, keepdims=True)
    return (centered * lax.rsqrt(variance + 1e-5) * norm_gain + norm_bias).astype(jnp.bfloat16)


def attend_block(q_blk, k_all, v_all):
    scale_f = 1.0 / math.sqrt(q_blk.shape[-1])
    scores = jnp.einsum('bqhd,bkhd->bhqk', q_blk, k_all, preferred_element_type=jnp.float32) * scale_f
    row_exp = jnp.exp(scores - scores.max(axis=-1, keepdims=True))
    row_sum = row_exp.sum(axis=-1)
    row_out = jnp.einsum('bhqk,bkhd->bqhd', row_exp.astype(jnp.bfloat16), v_all, preferred_element_type=jnp.float32)
    return (row_out / jnp.swapaxes(row_sum, 1, 2)[..., None]).astype(jnp.bfloat16)


def attend_rows(q_all, k_all, v_all, rows_n):
    batch_n, tok_n, head_n, dim_n = q_all.shape
    q_rows = jnp.swapaxes(q_all.reshape(batch_n, rows_n, tok_n // rows_n, head_n, dim_n), 0, 1)
    attended = lax.map(lambda q_row: attend_block(q_row, k_all, v_all), q_rows)
    return jnp.swapaxes(attended, 0, 1).reshape(batch_n, tok_n, head_n, dim_n)


def transformer_local(hidden, context, tr_norm, proj_w, proj_b, ln_par, self_qkv, cross_q, cross_kv, attn_out, attn_b, ff_in_w, ff_in_b, ff_out_w, ff_out_b, sp_size):
    batch_n, rows_n, cols_n, chan_n = hidden.shape
    normed = group_norm_sp(hidden, tr_norm[0], tr_norm[1], 1e-6, sp_size).astype(jnp.bfloat16).reshape(batch_n, rows_n * cols_n, chan_n)
    hidden_tok = (jnp.einsum('bnc,cd->bnd', normed, proj_w[0], preferred_element_type=jnp.float32) + proj_b[0]).astype(jnp.bfloat16)
    ff_width = ff_out_w.shape[1]
    for layer_i in range(ln_par.shape[0]):
        normed = layer_norm(hidden_tok, ln_par[layer_i, 0, 0], ln_par[layer_i, 0, 1])
        qkv_loc = jnp.einsum('bnc,jchd->jbnhd', normed, self_qkv[layer_i], preferred_element_type=jnp.float32).astype(jnp.bfloat16)
        qkv_heads = lax.all_to_all(qkv_loc, 'sp', 3, 2, tiled=True)
        attended = attend_rows(qkv_heads[0], qkv_heads[1], qkv_heads[2], rows_n * sp_size)
        att_rows = lax.all_to_all(attended, 'sp', 1, 2, tiled=True)
        hidden_tok = (hidden_tok.astype(jnp.float32) + jnp.einsum('bnhd,hdc->bnc', att_rows, attn_out[layer_i, 0], preferred_element_type=jnp.float32) + attn_b[layer_i, 0]).astype(jnp.bfloat16)
        normed = layer_norm(hidden_tok, ln_par[layer_i, 1, 0], ln_par[layer_i, 1, 1])
        q_cross = jnp.einsum('bnc,chd->bnhd', normed, cross_q[layer_i], preferred_element_type=jnp.float32).astype(jnp.bfloat16)
        kv_cross = jnp.einsum('btc,jchd->jbthd', context, cross_kv[layer_i], preferred_element_type=jnp.float32).astype(jnp.bfloat16)
        crossed = attend_block(q_cross, kv_cross[0], kv_cross[1])
        hidden_tok = (hidden_tok.astype(jnp.float32) + jnp.einsum('bnhd,hdc->bnc', crossed, attn_out[layer_i, 1], preferred_element_type=jnp.float32) + attn_b[layer_i, 1]).astype(jnp.bfloat16)
        normed = layer_norm(hidden_tok, ln_par[layer_i, 2, 0], ln_par[layer_i, 2, 1])
        ff_proj = jnp.einsum('bnc,cf->bnf', normed, ff_in_w[layer_i], preferred_element_type=jnp.float32) + ff_in_b[layer_i]
        gated_act = (ff_proj[..., :ff_width] * jax.nn.gelu(ff_proj[..., ff_width:], approximate=False)).astype(jnp.bfloat16)
        hidden_tok = (hidden_tok.astype(jnp.float32) + jnp.einsum('bnf,fc->bnc', gated_act, ff_out_w[layer_i], preferred_element_type=jnp.float32) + ff_out_b[layer_i]).astype(jnp.bfloat16)
    out_tok = jnp.einsum('bnc,cd->bnd', hidden_tok, proj_w[1], preferred_element_type=jnp.float32) + proj_b[1] + hidden.reshape(batch_n, rows_n * cols_n, chan_n).astype(jnp.float32)
    return out_tok.astype(jnp.bfloat16).reshape(batch_n, rows_n, cols_n, chan_n)


def device_block(latents, time_emb, context, res_norm, res_conv_w, res_conv_b, res_temb_w, res_temb_b, tr_norm, proj_w, proj_b, ln_par, self_qkv, cross_q, cross_kv, attn_out, attn_b, ff_in_w, ff_in_b, ff_out_w, ff_out_b, sp_size):
    first_out = resnet_local(latents, time_emb, 0, res_norm, res_conv_w, res_conv_b, res_temb_w, res_temb_b, sp_size)
    middle = transformer_local(first_out, context, tr_norm, proj_w, proj_b, ln_par, self_qkv, cross_q, cross_kv, attn_out, attn_b, ff_in_w, ff_in_b, ff_out_w, ff_out_b, sp_size)
    return resnet_local(middle, time_emb, 1, res_norm, res_conv_w, res_conv_b, res_temb_w, res_temb_b, sp_size)


def solution(mesh):
    sp_size = mesh.shape['sp']
    row_spec = P('dp', 'sp')
    part_spec = P('dp')
    in_specs = (row_spec, part_spec, part_spec) + (P(),) * 18
    body_fn = functools.partial(device_block, sp_size=sp_size)
    return jax.shard_map(body_fn, mesh=mesh, in_specs=in_specs, out_specs=row_spec, check_vma=False)
```

profile of v0, /device:TPU:0, one launch (start us, length us, event | category | flops | bytes accessed | tf_op | source)
XLA Modules:
  0.0 2084.6 jit_solution(14551654775584876145)
XLA Ops:
  30.7 12.5 copy.364
  60.2 60.3 %fusion.461 = (f32[2,48,17,1280]{3,1,2,0:T(8,128)}, f32[2,48,17,1280]{3,1,2,0:T(8,128)S(1)}) fusion(f32[2,48,17,1280]{3,0,2,1:T(2,128)} %bitcast.553, f32[1280]{0:T(1024)S(1)} %get-tuple-element.149, bf16[2,2,3,3,1280,1280]{5,4,3,2,1,0:T(8,128)(2,1)} %param.29, bf16[4,6,8,19,1280]{4,0,3,2,1:T(4,128)(2,1)} %fusion.118, pred[48,17]{0,1:T(8,128)(4,1)S(1)} %copy-done.59), kind=kOutput, calls=%fused_computation.511 | convolution fusion | flops 48142172160 | bytes 63903536 | tf_op jit(solution)/shard_map/conv_general_dilated | solution.py:30
  135.3 13.3 copy.299
  150.3 26.3 %psum.36 = f32[2,6,32]{2,1,0:T(8,128)S(1)} all-reduce(f32[2,6,32]{2,1,0:T(8,128)S(1)} %pad_maximum_fusion.1), channel_id=1, replica_groups=mesh['dp'=4,'sp'=4] {'sp'}, use_global_device_ids=true, to_apply=%region_9.10 | all-reduce | flops 384 | bytes 3072 | tf_op jit(solution)/shard_map/psum | solution.py:15
  243.6 13.4 maximum_bitcast_fusion.1
  265.3 55.9 %select_add_fusion.1 = f32[2,48,17,1280]{3,1,2,0:T(8,128)} fusion(bf16[2,2,3,3,1280,1280]{5,4,3,2,1,0:T(8,128)(2,1)} %param.29, bf16[4,6,8,19,1280]{4,0,3,2,1:T(4,128)(2,1)S(1)} %fusion.119, f32[1280]{0:T(1024)S(1)} %copy-done.55, pred[48,17]{0,1:T(8,128)(4,1)S(1)} %copy-done.59), kind=kOutput, calls=%fused_computation.177 | convolution fusion | flops 48133816320 | bytes 47191856 | tf_op jit(solution)/shard_map/conv_general_dilated | solution.py:30
  321.2 14.7 copy.309
  352.5 14.5 psum.37
  379.9 22.8 %convert_bitcast_fusion.1 = bf16[3,6,256,20,64]{2,4,3,0,1:T(8,128)(2,1)} fusion(bf16[2,3,1280,20,64]{2,4,3,1,0:T(8,128)(2,1)} %param.37, bf16[6,256,1280]{2,1,0:T(8,128)(2,1)S(1)} %get-tuple-element.211, f32[1280]{0:T(1024)S(1)} %copy-done.44, f32[1280]{0:T(1024)S(1)} %copy-done.45, f32[6,256]{1,0:T(8,128)S(1)} %add_rsqrt_fusion.5, ...), kind=kOutput, calls=%fused_computation.125 | convolution fusion | flops 15117189120 | bytes 25581568 | tf_op jit(solution)/shard_map/bnc,jchd->jbnhd/dot_general | solution.py:72
  419.5 129.3 %all-to-all-done = bf16[3,6,256,20,64]{2,4,0,1,3:T(8,128)(2,1)} async-done(((bf16[3,6,256,20,64]{2,4,0,1,3:T(8,128)(2,1)}), bf16[3,6,256,20,64]{2,4,0,1,3:T(8,128)(2,1)}, u32[]{:S(2)}, u32[]{:S(2)}) %all-to-all-start) | async-done | bytes 11796512 | tf_op jit(solution)/shard_map/all_to_all | solution.py:73
  548.8 13.8 copy.466
  600.9 164.5 %while.20 = (s32[]{:T(128)}, bf16[8,6,128,5,64]{2,4,3,1,0:T(8,128)(2,1)}, bf16[8,6,128,5,64]{2,4,3,1,0:T(8,128)(2,1)}, bf16[6,1024,5,64]{1,3,2,0:T(8,128)(2,1)}, bf16[6,1024,5,64]{1,3,2,0:T(8,128)(2,1)}, /*index=5*/s32[]{:T(128)}) while((s32[]{:T(128)}, bf16[8,6,128,5,64]{2,4,3,1,0:T(8,128)(2,1)}, bf16[8,6,128,5,64]{2,4,3,1,0:T(8,128)(2,1)}, ...), condition=%wide.region_20.21_spmd, body=%wide.region_17.20_spmd.sunk | while | flops 1038574080 | bytes 119025760 | solution.py:61
  801.6 34.7 %all-to-all-done.1 = bf16[4,2,245760]{2,1,0:T(2,128)(2,1)} async-done(((bf16[4,2,245760]{2,1,0:T(2,128)(2,1)}), bf16[4,2,245760]{2,1,0:T(2,128)(2,1)}, u32[]{:S(2)}, u32[]{:S(2)}) %all-to-all-start.1) | async-done | bytes 3932192 | tf_op jit(solution)/shard_map/all_to_all | solution.py:75
  872.7 14.4 multiply_reduce_fusion.3
  893.4 13.8 convert_reduce_fusion.4
  910.6 53.4 %broadcast_add_fusion.1 = f32[6,256,10240]{2,1,0:T(8,128)} fusion(f32[10240]{0:T(1024)S(1)} %bitcast.563, bf16[2,1280,10240]{2,1,0:T(8,128)(2,1)} %param.42, bf16[6,256,1280]{2,1,0:T(8,128)(2,1)} %get-tuple-element.217, f32[1280]{0:T(1024)S(1)} %copy-done.40, f32[1280]{0:T(1024)S(1)} %copy-done.41, f32[6,256]{1,0:T(8,128)S(1)} %add_rsqrt_fusion.3, ...), kind=kOutput, calls=%fused_computation.69 | convolution fusion | flops 40292843520 | bytes 93124608 | tf_op jit(solution)/shard_map/bnc,cf->bnf/dot_general | solution.py:83
  964.0 96.4 %convert_reduce_fusion.3 = (f32[6,256]{1,0:T(8,128)S(1)}, bf16[6,256,1280]{2,1,0:T(8,128)(2,1)S(1)}) fusion(f32[1280]{0:T(1024)S(1)} %copy-done.50, bf16[2,5120,1280]{2,1,0:T(8,128)(2,1)} %param.44, f32[6,256,10240]{2,1,0:T(8,128)} %broadcast_add_fusion.1, bf16[6,256,1280]{2,1,0:T(8,128)(2,1)S(1)} %copy-done.18), kind=kOutput, calls=%fused_computation.118 | convolution fusion | flops 20663498752 | bytes 83897344 | tf_op jit(solution)/shard_map/bnf,fc->bnc/dot_general | solution.py:85
  1061.7 22.8 %convert_bitcast_fusion = bf16[3,6,256,20,64]{2,4,3,0,1:T(8,128)(2,1)} fusion(bf16[2,3,1280,20,64]{2,4,3,1,0:T(8,128)(2,1)} %param.37, bf16[6,256,1280]{2,1,0:T(8,128)(2,1)S(1)} %get-tuple-element.219, f32[1280]{0:T(1024)S(1)} %copy-done.38, f32[1280]{0:T(1024)S(1)} %copy-done.39, f32[6,256]{1,0:T(8,128)S(1)} %add_rsqrt_fusion.2, ...), kind=kOutput, calls=%fused_computation.115 | convolution fusion | flops 15117189120 | bytes 25581568 | tf_op jit(solution)/shard_map/bnc,jchd->jbnhd/dot_general | solution.py:72
  1090.5 132.7 %all_to_all.66 = bf16[3,6,256,20,64]{2,4,0,1,3:T(8,128)(2,1)S(1)} all-to-all(bf16[3,6,256,20,64]{2,4,0,1,3:T(8,128)(2,1)S(1)} %copy.320), channel_id=1, replica_groups=mesh['dp'=4,'sp'=4] {'sp'}, dimensions={3} | all-to-all | bytes 23592960 | tf_op jit(solution)/shard_map/all_to_all | solution.py:73
  1271.6 164.5 %while.21 = (s32[]{:T(128)}, bf16[8,6,128,5,64]{2,4,3,1,0:T(8,128)(2,1)}, bf16[8,6,128,5,64]{2,4,3,1,0:T(8,128)(2,1)}, bf16[6,1024,5,64]{1,3,2,0:T(8,128)(2,1)}, bf16[6,1024,5,64]{1,3,2,0:T(8,128)(2,1)}, /*index=5*/s32[]{:T(128)}) while((s32[]{:T(128)}, bf16[8,6,128,5,64]{2,4,3,1,0:T(8,128)(2,1)}, bf16[8,6,128,5,64]{2,4,3,1,0:T(8,128)(2,1)}, ...), condition=%wide.region_32.33_spmd, body=%wide.region_29.32_spmd.sunk | while | flops 1038574080 | bytes 119025760 | solution.py:61
  1470.2 36.6 %all-to-all-done.3 = bf16[4,2,245760]{2,1,0:T(2,128)(2,1)} async-done(((bf16[4,2,245760]{2,1,0:T(2,128)(2,1)}), bf16[4,2,245760]{2,1,0:T(2,128)(2,1)}, u32[]{:S(2)}, u32[]{:S(2)}) %all-to-all-start.3) | async-done | bytes 3932192 | tf_op jit(solution)/shard_map/all_to_all | solution.py:75
  1543.4 14.4 multiply_reduce_fusion.2
  1564.2 13.8 convert_reduce_fusion.1
  1581.3 54.1 %broadcast_add_fusion = f32[6,256,10240]{2,1,0:T(8,128)} fusion(f32[10240]{0:T(1024)S(1)} %bitcast.562, bf16[2,1280,10240]{2,1,0:T(8,128)(2,1)} %param.42, bf16[6,256,1280]{2,1,0:T(8,128)(2,1)} %get-tuple-element.225, f32[1280]{0:T(1024)S(1)} %copy-done.35, f32[1280]{0:T(1024)S(1)} %copy-done.34, f32[6,256]{1,0:T(8,128)S(1)} %add_rsqrt_fusion, ...), kind=kOutput, calls=%fused_computation.55 | convolution fusion | flops 40292843520 | bytes 93124608 | tf_op jit(solution)/shard_map/bnc,cf->bnf/dot_general | solution.py:83
  1635.5 96.1 %fusion.175 = bf16[6,256,1280]{2,1,0:T(8,128)(2,1)S(1)} fusion(bf16[6,256,1280]{2,1,0:T(8,128)(2,1)S(1)} %copy-done.17, bf16[2,5120,1280]{2,1,0:T(8,128)(2,1)} %param.44, f32[6,256,10240]{2,1,0:T(8,128)} %broadcast_add_fusion, f32[1280]{0:T(1024)S(1)} %copy-done.48), kind=kOutput, calls=%fused_computation.218 | convolution fusion | flops 20659568640 | bytes 83891200 | tf_op jit(solution)/shard_map/bnf,fc->bnc/dot_general | solution.py:85
  1764.0 12.5 copy.365
  1793.4 60.3 %fusion.478 = (f32[2,48,17,1280]{3,1,2,0:T(8,128)}, f32[2,48,17,1280]{3,1,2,0:T(8,128)S(1)}) fusion(f32[2,48,17,1280]{3,0,2,1:T(2,128)} %bitcast.554, f32[1280]{0:T(1024)S(1)} %copy-done.52, bf16[2,2,3,3,1280,1280]{5,4,3,2,1,0:T(8,128)(2,1)} %param.29, bf16[4,6,8,19,1280]{4,0,3,2,1:T(4,128)(2,1)} %fusion.120, pred[48,17]{0,1:T(8,128)(4,1)S(1)} %copy-done.60), kind=kOutput, calls=%fused_computation.512 | convolution fusion | flops 48142172160 | bytes 63903536 | tf_op jit(solution)/shard_map/conv_general_dilated | solution.py:30
  1868.5 13.3 copy.333
  1883.5 26.3 %psum.39 = f32[2,6,32]{2,1,0:T(8,128)S(1)} all-reduce(f32[2,6,32]{2,1,0:T(8,128)S(1)} %pad_maximum_fusion.4), channel_id=1, replica_groups=mesh['dp'=4,'sp'=4] {'sp'}, use_global_device_ids=true, to_apply=%region_48.49 | all-reduce | flops 384 | bytes 3072 | tf_op jit(solution)/shard_map/psum | solution.py:15
  1974.7 13.4 maximum_bitcast_fusion.3
  1996.4 56.0 %select_add_fusion = f32[2,48,17,1280]{3,1,2,0:T(8,128)} fusion(bf16[2,2,3,3,1280,1280]{5,4,3,2,1,0:T(8,128)(2,1)} %param.29, bf16[4,6,8,19,1280]{4,0,3,2,1:T(4,128)(2,1)S(1)} %fusion.121, f32[1280]{0:T(1024)S(1)} %copy-done.51, pred[48,17]{0,1:T(8,128)(4,1)S(1)} %copy-done.60), kind=kOutput, calls=%fused_computation.175 | convolution fusion | flops 48133816320 | bytes 47191856 | tf_op jit(solution)/shard_map/conv_general_dilated | solution.py:30
  2052.3 14.6 copy.343
  (408 shorter events, 926.2 us)
Async XLA Ops:
  0.0 791.2 %copy-start = (bf16[6,77,1024]{2,1,0:T(8,128)(2,1)S(1)}, bf16[6,77,1024]{2,1,0:T(8,128)(2,1)}, u32[]{:S(2)}) copy-start(bf16[6,77,1024]{2,1,0:T(8,128)(2,1)} %param.27) | copy-start | bytes 2838532
  19.4 5.1 collective-permute-start
  20.8 6.3 collective-permute-start.1
  211.1 23.0 %collective-permute-start.2 = (bf16[6,1,128,1280]{3,2,0,1:T(8,128)(2,1)}, bf16[6,1,128,1280]{3,2,0,1:T(8,128)(2,1)}, u32[]{:S(2)}, u32[]{:S(2)}) collective-permute-start(bf16[6,1,128,1280]{3,2,0,1:T(8,128)(2,1)} %slice_bitcast_fusion.9), channel_id=1, source_target_pairs={{0,1},{1,2},{2,3},{4,5},{5,6},{6,7},{8,9},{9,10},{10,11},{12,13},{... | collective-permute-start | bytes 5898248 | tf_op jit(solution)/shard_map/ppermute | solution.py:27
  220.5 18.2 collective-permute-start.3
  345.0 22.5 %copy-start.24 = (f32[1280]{0:T(1024)S(1)}, f32[1280]{0:T(1024)}, u32[]{:S(2)}) copy-start(f32[1280]{0:T(1024)} %get-tuple-element.161) | copy-start | bytes 15364
  345.0 22.5 %copy-start.25 = (f32[1280]{0:T(1024)S(1)}, f32[1280]{0:T(1024)}, u32[]{:S(2)}) copy-start(f32[1280]{0:T(1024)} %get-tuple-element.162) | copy-start | bytes 15364
  352.1 18.9 copy-start.49
  378.7 24.0 %copy-start.11 = (bf16[6,256,1280]{2,1,0:T(8,128)(2,1)}, bf16[6,256,1280]{2,1,0:T(8,128)(2,1)S(1)}, u32[]{:S(2)}) copy-start(bf16[6,256,1280]{2,1,0:T(8,128)(2,1)S(1)} %get-tuple-element.211) | copy-start | bytes 11796484
  413.0 135.8 %all-to-all-start = ((bf16[3,6,256,20,64]{2,4,0,1,3:T(8,128)(2,1)}), bf16[3,6,256,20,64]{2,4,0,1,3:T(8,128)(2,1)}, u32[]{:S(2)}, u32[]{:S(2)}) async-start(bf16[3,6,256,20,64]{2,4,0,1,3:T(8,128)(2,1)} %copy.311), calls=%async_computation | async-start | bytes 23592960 | tf_op jit(solution)/shard_map/all_to_all | solution.py:73
  786.4 49.9 %all-to-all-start.1 = ((bf16[4,2,245760]{2,1,0:T(2,128)(2,1)}), bf16[4,2,245760]{2,1,0:T(2,128)(2,1)}, u32[]{:S(2)}, u32[]{:S(2)}) async-start(bf16[4,2,245760]{2,1,0:T(2,128)(2,1)} %reshape.410), calls=%async_computation.1 | async-start | bytes 7864320 | tf_op jit(solution)/shard_map/all_to_all | solution.py:75
  893.4 17.2 copy-start.40
  893.4 17.2 copy-start.41
  910.6 53.4 %copy-start.18 = (bf16[6,256,1280]{2,1,0:T(8,128)(2,1)S(1)}, bf16[6,256,1280]{2,1,0:T(8,128)(2,1)}, u32[]{:S(2)}) copy-start(bf16[6,256,1280]{2,1,0:T(8,128)(2,1)} %get-tuple-element.217) | copy-start | bytes 11796484
  910.6 53.4 %copy-start.50 = (f32[1280]{0:T(1024)S(1)}, f32[1280]{0:T(1024)}, u32[]{:S(2)}) copy-start(f32[1280]{0:T(1024)} %get-tuple-element.160) | copy-start | bytes 15364
  964.0 97.7 %copy-start.38 = (f32[1280]{0:T(1024)S(1)}, f32[1280]{0:T(1024)}, u32[]{:S(2)}) copy-start(f32[1280]{0:T(1024)} %get-tuple-element.130) | copy-start | bytes 15364
  964.0 97.7 %copy-start.39 = (f32[1280]{0:T(1024)S(1)}, f32[1280]{0:T(1024)}, u32[]{:S(2)}) copy-start(f32[1280]{0:T(1024)} %get-tuple-element.131) | copy-start | bytes 15364
  1060.4 24.1 %copy-start.13 = (bf16[6,256,1280]{2,1,0:T(8,128)(2,1)}, bf16[6,256,1280]{2,1,0:T(8,128)(2,1)S(1)}, u32[]{:S(2)}) copy-start(bf16[6,256,1280]{2,1,0:T(8,128)(2,1)S(1)} %get-tuple-element.219) | copy-start | bytes 11796484
  1457.0 49.9 %all-to-all-start.3 = ((bf16[4,2,245760]{2,1,0:T(2,128)(2,1)}), bf16[4,2,245760]{2,1,0:T(2,128)(2,1)}, u32[]{:S(2)}, u32[]{:S(2)}) async-start(bf16[4,2,245760]{2,1,0:T(2,128)(2,1)} %reshape.412), calls=%async_computation.3 | async-start | bytes 7864320 | tf_op jit(solution)/shard_map/all_to_all | solution.py:75
  1564.2 17.1 copy-start.21
  1564.2 17.1 copy-start.34
  1564.2 17.1 copy-start.35
  1581.3 54.1 %copy-start.17 = (bf16[6,256,1280]{2,1,0:T(8,128)(2,1)S(1)}, bf16[6,256,1280]{2,1,0:T(8,128)(2,1)}, u32[]{:S(2)}) copy-start(bf16[6,256,1280]{2,1,0:T(8,128)(2,1)} %get-tuple-element.225) | copy-start | bytes 11796484
  1581.3 54.1 %copy-start.48 = (f32[1280]{0:T(1024)S(1)}, f32[1280]{0:T(1024)}, u32[]{:S(2)}) copy-start(f32[1280]{0:T(1024)} %get-tuple-element.159) | copy-start | bytes 15364
  1635.5 96.1 %copy-start.10 = (bf16[6,2,128,1280]{3,2,1,0:T(8,128)(2,1)S(1)}, bf16[6,2,128,1280]{3,2,1,0:T(8,128)(2,1)}, u32[]{:S(2)}) copy-start(bf16[6,2,128,1280]{3,2,1,0:T(8,128)(2,1)} %get-tuple-element.183) | copy-start | bytes 11796484
  1635.5 96.1 %copy-start.47 = (f32[1280]{0:T(1024)S(1)}, f32[1280]{0:T(1024)}, u32[]{:S(2)}) copy-start(f32[1280]{0:T(1024)} %get-tuple-element.157) | copy-start | bytes 15364
  1635.5 96.1 %copy-start.56 = (bf16[2,1280,1280]{2,1,0:T(8,128)(2,1)S(1)}, bf16[2,1280,1280]{2,1,0:T(8,128)(2,1)}, u32[]{:S(2)}) copy-start(bf16[2,1280,1280]{2,1,0:T(8,128)(2,1)} %param.34) | copy-start | bytes 19660804
  1751.4 5.2 collective-permute-start.4
  1753.1 6.8 collective-permute-start.5
  1944.3 20.8 %collective-permute-start.6 = (bf16[6,1,128,1280]{3,2,0,1:T(8,128)(2,1)}, bf16[6,1,128,1280]{3,2,0,1:T(8,128)(2,1)}, u32[]{:S(2)}, u32[]{:S(2)}) collective-permute-start(bf16[6,1,128,1280]{3,2,0,1:T(8,128)(2,1)} %slice_bitcast_fusion.3), channel_id=1, source_target_pairs={{0,1},{1,2},{2,3},{4,5},{5,6},{6,7},{8,9},{9,10},{10,11},{12,13},{... | collective-permute-start | bytes 5898248 | tf_op jit(solution)/shard_map/ppermute | solution.py:27
  1953.7 16.2 collective-permute-start.7
  2066.9 17.4 copy-start.1
  (58 other events, 432.4 us)
where the time goes:
time: 2100 us; the launch traced here: 2080 us
  matrix products  922 us (44%)
  local copies, waits for them, and re-layouts  499 us (24%)
  blocking collectives  214 us (10%)
  other arithmetic  208 us (10%)
  waiting for transfers between devices  208 us (10%)
  starting transfers between devices  30.6 us (1%)
    conv_general_dilated x4, matrix products, conv_rows(): lax.conv_general_dilated(padded, kernel, (1, 1), ((0, 0), (1, 1)), dimens...  232 us
    dot_general x2, matrix products, transformer_local(): jnp.einsum('bnf,fc->bnc', gated_act, ff_out_w[layer_i], preferred_element...  193 us
    dot_general x16, matrix products, attend_block(): jnp.einsum('bhqk,bkhd->bqhd', row_exp.astype(jnp.bfloat16), v_all, prefer...  167 us
    all_to_all x1, blocking collectives, transformer_local(): qkv_heads = lax.all_to_all(qkv_loc, 'sp', 3, 2, tiled=True)  133 us
    all_to_all x1, waiting for transfers between devices, transformer_local(): qkv_heads = lax.all_to_all(qkv_loc, 'sp', 3, 2, tiled=True)  129 us
    dot_general x2, matrix products, transformer_local(): jnp.einsum('bnc,cf->bnf', normed, ff_in_w[layer_i], preferred_element_typ...  108 us
    dot_general x18, matrix products, attend_block(): jnp.einsum('bqhd,bkhd->bhqk', q_blk, k_all, preferred_element_type=jnp.fl...  103 us
    psum x5, blocking collectives, group_norm_sp(): total_sums = lax.psum(local_sums, 'sp')  81.8 us
  transfers between devices with their start and end apart: 11, of which 6 were waited for; matrix products, arithmetic and copies ran while one was open for 3% of the time, Pallas kernels for 0%

commit v1 on v0

v1 whole, which is shorter than its diff:
```python
import functools
import math
import jax
import jax.numpy as jnp
from jax import lax
from jax.experimental import pallas as pl
from jax.experimental.pallas import tpu as pltpu
from jax.sharding import PartitionSpec as P

F32 = jnp.float32
BF = jnp.bfloat16
HIGHEST = lax.Precision.HIGHEST
NT = (((1,), (1,)), ((), ()))
NUM_GROUPS = 32
HEAD = 64
LANES = 128
MIB = 2 ** 20
LATENTS = 3
KERNEL = 3
WIDE = 256
SUM_ROWS = 8
CTX_ROWS = 80
SOFTMAX_MUL = math.log2(math.e) / math.sqrt(HEAD)

def params(mib):
    return pltpu.CompilerParams(vmem_limit_bytes=mib * MIB)


def cost(flops, nbytes):
    return pl.CostEstimate(flops=int(flops), bytes_accessed=int(nbytes), transcendentals=0)


def fixed(shape, *lead):
    index = tuple(lead) + (0,) * (len(shape) - len(lead))
    return pl.BlockSpec(tuple(shape), lambda *_: index, pipeline_mode=pl.Buffered(1))


def whole(array):
    return fixed(array.shape)


def major(shape):
    return pl.BlockSpec(tuple(shape), lambda b, *_: (b,) + (0,) * (len(shape) - 1))


def minor(shape, lead=0):
    return pl.BlockSpec(tuple(shape), lambda n, *_: (lead,) + (0,) * (len(shape) - 2) + (n,))


def any_space():
    return pl.BlockSpec(memory_space=pl.ANY)


def dot(left, right):
    return jnp.dot(left, right, preferred_element_type=F32)


def dot_nt(left, right):
    return lax.dot_general(left, right, NT, preferred_element_type=F32)


def col_sum(values):
    return jnp.sum(values, axis=0, keepdims=True)


def col_max(values):
    return jnp.max(values, axis=0, keepdims=True)


def row_of(ref, *index):
    return ref[index][None, :]


def affine(ref, *index):
    return row_of(ref, *index, 0), row_of(ref, *index, 1)


def like(array, dtype=BF):
    return jax.ShapeDtypeStruct(tuple(array), dtype)


def at_lanes(index, size=LANES):
    return slice(index * size, (index + 1) * size)


def pairs_of(text):
    return [tuple(map(int, pair)) for pair in text.split()]


def group_stats(totals, lat, count, eps):
    chan = totals.shape[1]
    per = chan // NUM_GROUPS
    fold = (lax.broadcasted_iota(jnp.int32, (chan, LANES), 0) // per == lax.broadcasted_iota(jnp.int32, (chan, LANES), 1)).astype(F32)
    spread = (lax.broadcasted_iota(jnp.int32, (LANES, chan), 1) // per == lax.broadcasted_iota(jnp.int32, (LANES, chan), 0)).astype(F32)
    grouped = jnp.dot(totals, fold, precision=HIGHEST, preferred_element_type=F32) * (1.0 / (count * per))
    means = jnp.dot(grouped, spread, precision=HIGHEST, preferred_element_type=F32)
    mean = means[0:lat]
    return mean, lax.rsqrt(means[lat:2 * lat] - mean * mean + eps)


def layer_norm(values, gain, bias):
    centered = values - jnp.mean(values, axis=-1, keepdims=True)
    variance = jnp.mean(centered * centered, axis=-1, keepdims=True)
    return (centered * lax.rsqrt(variance + 1e-5) * gain + bias).astype(BF)


def place_rows(sums, squares, base):
    zero = jnp.zeros_like(sums[0])
    rows = [zero] * SUM_ROWS
    for l, (one, two) in enumerate(zip(sums, squares)):
        rows[base + l] = one
        rows[LATENTS + base + l] = two
    return jnp.concatenate(rows, axis=0)


def conv_kernel(core_ref, v_ref, halo_ref, own_ref, peer_ref, norm_ref, bias_ref, *rest, res_i, conv_i, eps, base, has_temb, has_res, has_into, want_sums):
    rest = list(rest)
    temb_ref = rest.pop(0) if has_temb else None
    w_hbm = rest.pop(0)
    res_ref = rest.pop(0) if has_res else None
    acat, w_buf, w_sem = rest[-3:]
    rest = rest[:-3]
    before_ref = None
    if has_into:
        _, _, before_ref = rest[:3]
        rest = rest[3:]
    out_ref = rest.pop(0)
    sum_ref, edge_ref = rest if want_sums else (None, None)
    lat, tok, chan = v_ref.shape
    rows = tok // LANES
    core = core_ref[0]
    step, steps = pl.program_id(0), pl.num_programs(0)
    nt = out_ref.shape[-1]

    def fetch(n):
        lanes = pl.ds(pl.multiple_of(n * nt, LANES), nt)
        return pltpu.make_async_copy(w_hbm.at[2 * res_i + conv_i, :, :, lanes], w_buf.at[n % 2], w_sem.at[n % 2])

    @pl.when(step == 0)
    def _():
        fetch(0).start()
        fetch(1).start()
        mean, inv = group_stats(own_ref[...] + peer_ref[...], LATENTS, 2 * tok, eps)
        gain, shift = affine(norm_ref, res_i, conv_i)
        scale = inv * gain

        def emit(src, l, row, cs):
            g = base + l
            x = (src.astype(F32) - row_of(mean, g, cs)) * row_of(scale, g, cs) + shift[:, cs]
            half = 0.5 * x
            y = half * jnp.tanh(half) + half
            col = lax.broadcasted_iota(jnp.int32, y.shape, 0)
            left = jnp.where(col == 0, 0.0, pltpu.roll(y, 1, 0))
            right = jnp.where(col == LANES - 1, 0.0, pltpu.roll(y, LANES - 1, 0))
            rr = pl.ds(pl.multiple_of(row * LANES, LANES), LANES)
            for d, val in enumerate((left, y, right)):
                acat[l, rr, d * chan + cs.start:d * chan + cs.stop] = val.astype(BF)

        for l in range(lat):
            def one_row(r, carry):
                for ch in range(chan // WIDE):
                    cs = at_lanes(ch, WIDE)
                    emit(v_ref[l, pl.ds(pl.multiple_of(r * LANES, LANES), LANES), cs], l, r + 1, cs)
                return carry

            lax.fori_loop(0, rows, one_row, 0)
            for ch in range(chan // WIDE):
                cs = at_lanes(ch, WIDE)
                emit(halo_ref[l, :, cs], l, jnp.where(core == 0, rows + 1, 0), cs)
            rr = pl.ds(pl.multiple_of(jnp.where(core == 0, 0, rows + 1) * LANES, LANES), LANES)
            acat[l, rr, :] = jnp.zeros((LANES, KERNEL * chan), BF)

    slot = step % 2
    fetch(step).wait()
    sums, squares = [], []
    for l in range(lat):
        acc = row_of(bias_ref, res_i, conv_i)
        for dy in range(KERNEL):
            acc += dot(acat[l, dy * LANES:tok + dy * LANES, :], w_buf[slot, dy])
        if has_temb:
            acc += row_of(temb_ref, base + l)
        if has_res:
            acc += res_ref[l].astype(F32)
        out = acc.astype(BF)
        out_ref[l] = out
        if want_sums:
            edge_ref[l] = jnp.where(core == 0, out[tok - LANES:], out[:LANES])
            out = out.astype(F32)
            sums.append(col_sum(out))
            squares.append(col_sum(out * out))
    if want_sums:
        placed = place_rows(sums, squares, base)
        sum_ref[...] = placed + before_ref[...] if has_into else placed

    @pl.when(step + 2 < steps)
    def _():
        fetch(step + 2).start()


def conv_call(core, v, halo, own, peer, norm, bias, weights, res_i, conv_i, temb=None, res=None, into=None, base=0, lat=LATENTS, want_sums=True, nt=256):
    tok, chan = v.shape[1:]
    pick = lambda a: (base // lat if a.shape[0] > lat else 0)
    rows = lambda a: fixed((lat,) + a.shape[1:], pick(a))
    tile = lambda a, size: minor((lat, size, nt), pick(a))
    specs = [rows(v), rows(halo), whole(own), whole(peer), whole(norm), minor(bias.shape[:-1] + (nt,))]
    args = [v, halo, own, peer, norm, bias]
    if temb is not None:
        specs.append(minor((LATENTS, nt)))
        args.append(temb)
    specs.append(any_space())
    args.append(weights)
    if res is not None:
        specs.append(tile(res, tok))
        args.append(res)
    aliases = {}
    held = LATENTS if want_sums else lat
    out = like((held, tok, chan))
    if into is not None:
        aliases = {len(args) + 1: 0, len(args) + 2: 2}
        specs += [any_space(), any_space(), minor((SUM_ROWS, nt))]
        args += [into[0], into[2], into[1]]
    out_specs, out_shape = [tile(out, tok)], [out]
    if want_sums:
        out_specs += [minor((SUM_ROWS, nt)), tile(out, LANES)]
        out_shape += [like((SUM_ROWS, chan), F32), like((held, LANES, chan))]
    body = functools.partial(conv_kernel, res_i=res_i, conv_i=conv_i, eps=1e-5, base=base, has_temb=temb is not None, has_res=res is not None, has_into=into is not None, want_sums=want_sums)
    outs = pl.pallas_call(
        body,
        grid_spec=pltpu.PrefetchScalarGridSpec(
            num_scalar_prefetch=1, grid=(chan // nt,), in_specs=specs, out_specs=out_specs,
            scratch_shapes=[pltpu.VMEM((lat, tok + 2 * LANES, KERNEL * chan), BF), pltpu.VMEM((2, KERNEL, KERNEL * chan, nt), BF), pltpu.SemaphoreType.DMA((2,))]),
        out_shape=out_shape, compiler_params=params(60), input_output_aliases=aliases,
        cost_estimate=cost(18 * lat * tok * chan * chan, 18 * chan * chan), name="conv")(core, *args)
    return outs if want_sums else outs[0]


def gather_kernel(where_ref, own_ref, *rest, base, lat, has_into):
    firsts, seconds = rest[:lat], rest[lat:2 * lat]
    v_ref, sum_ref, edge_ref = rest[2 * lat + has_into:]
    index = where_ref[0]
    chip, core = index // 2, index % 2
    half = own_ref.shape[1]
    mine = jnp.logical_or(index == 0, index == 3)
    sums, squares = [], []
    for l in range(lat):
        third = jnp.where(mine, own_ref[l], seconds[l][0])
        first = firsts[l][0]
        top = jnp.where(chip == 0, third, first)
        bottom = jnp.where(chip == 0, first, third)
        v_ref[l, 0:half] = top
        v_ref[l, half:] = bottom
        edge_ref[l] = jnp.where(core == 0, bottom[half - LANES:], top[:LANES])
        top, bottom = top.astype(F32), bottom.astype(F32)
        sums.append(col_sum(top) + col_sum(bottom))
        squares.append(col_sum(top * top) + col_sum(bottom * bottom))
    sum_ref[...] = place_rows(sums, squares, base)


def gather_call(where, flat, firsts, seconds, base, into=None):
    lat = len(firsts)
    half, chan = flat.shape[1:]
    nt = 640
    part = minor((1, half, nt))
    specs = [pl.BlockSpec((pl.Element(lat), pl.Element(half), pl.Element(nt)), lambda n, w: (w[0] // 2 * LATENTS + base, 0, n * nt))] + [part] * (2 * lat)
    args = [flat, *firsts, *seconds]
    aliases = {}
    if into is not None:
        specs.append(any_space())
        args.append(into)
        aliases = {len(args): 0}
    return pl.pallas_call(
        functools.partial(gather_kernel, base=base, lat=lat, has_into=into is not None),
        grid_spec=pltpu.PrefetchScalarGridSpec(
            num_scalar_prefetch=1, grid=(chan // nt,), in_specs=specs,
            out_specs=[minor((lat, 2 * half, nt), base // lat), minor((SUM_ROWS, nt)), minor((lat, LANES, nt))]),
        out_shape=[like((LATENTS, 2 * half, chan)), like((SUM_ROWS, chan), F32), like((lat, LANES, chan))],
        input_output_aliases=aliases, compiler_params=params(60), cost_estimate=cost(MIB, 8 * lat * half * chan), name="gather")(where, *args)


def enter_kernel(h_ref, own_ref, peer_ref, norm_ref, pw_ref, pb_ref, ln_ref, wk_ref, u_ref, n_ref, k_ref, mean_s, scale_s):
    step = pl.program_id(0)
    lat = pl.num_programs(0)

    @pl.when(step == 0)
    def _():
        mean, inv = group_stats(own_ref[...] + peer_ref[...], LATENTS, 2 * h_ref.shape[1], 1e-6)
        mean_s[:LATENTS] = mean
        scale_s[:LATENTS] = inv * row_of(norm_ref, 0)

    mean, scale = mean_s[pl.ds(step, 1), :], scale_s[pl.ds(step, 1), :]
    normed = ((h_ref[0].astype(F32) - mean) * scale + row_of(norm_ref, 1)).astype(BF)
    u = (dot(normed, pw_ref[0]) + row_of(pb_ref, 0)).astype(BF)
    u_ref[0] = u
    n = layer_norm(u.astype(F32), *affine(ln_ref, 0, 0))
    n_ref[0] = n
    k_ref[0] = dot_nt(n, wk_ref[0, 0]).astype(BF)


def enter_call(h, own, peer, tr_norm, proj_w, proj_b, ln_par, qkv_t):
    lat, tok, chan = h.shape
    row = major((1, tok, chan))
    return pl.pallas_call(
        enter_kernel, grid=(lat,),
        in_specs=[row, whole(own), whole(peer), whole(tr_norm), fixed((1, chan, chan)), whole(proj_b), whole(ln_par), fixed((1, 1, chan, chan), 0, 1)],
        out_specs=[row] * 3, out_shape=[like(h.shape)] * 3,
        scratch_shapes=[pltpu.VMEM((SUM_ROWS, chan), F32)] * 2,
        compiler_params=params(60), cost_estimate=cost(4 * lat * tok * chan * chan, 4 * chan * chan), name="enter")(
            h, own, peer, tr_norm, proj_w, proj_b, ln_par, qkv_t)


def key_kernel(u_ref, ln_ref, wk_ref, n_ref, k_ref, *, layer):
    n = layer_norm(u_ref[0].astype(F32), *affine(ln_ref, layer, 0))
    n_ref[0] = n
    k_ref[0] = dot_nt(n, wk_ref[0, 0]).astype(BF)


def key_call(u, ln_par, qkv_t, layer):
    lat, tok, chan = u.shape
    row = major((1, tok, chan))
    return pl.pallas_call(
        functools.partial(key_kernel, layer=layer), grid=(lat,),
        in_specs=[row, whole(ln_par), fixed((1, 1, chan, chan), layer, 1)],
        out_specs=[row] * 2, out_shape=[like(u.shape)] * 2,
        compiler_params=params(60), cost_estimate=cost(2 * lat * tok * chan * chan, 2 * chan * chan), name="keys")(u, ln_par, qkv_t)


def query_kernel(n_ref, w_ref, q_ref):
    q_ref[0] = dot_nt(n_ref[0], w_ref[0, 0]).astype(BF)


def value_kernel(n_ref, w_ref, v_ref):
    v_ref[0] = dot_nt(w_ref[0, 0], n_ref[0]).astype(BF)


def linear_call(kernel, n, qkv_t, layer, part, out_block, name):
    lat, tok, chan = n.shape
    return pl.pallas_call(
        kernel, grid=(lat,),
        in_specs=[major((1, tok, chan)), fixed((1, 1, chan, chan), layer, part)],
        out_specs=major((1,) + out_block), out_shape=like((lat,) + out_block),
        compiler_params=params(60), cost_estimate=cost(tok * chan * chan // 4, 2 * chan * chan), name=name)(n, qkv_t)


def attn_kernel(q_ref, k0_ref, k1_ref, v0_ref, v1_ref, o_ref, *, pairs):
    def scores(i):
        p, h = divmod(i, 2)
        ls = slice(p * LANES, (p + 1) * LANES)
        q = q_ref[0, :, ls]
        lane = lax.broadcasted_iota(jnp.int32, q.shape, 1)
        qh = jnp.where((lane >= HEAD) == (h == 1), q, jnp.zeros_like(q))
        return [dot_nt(k_ref[0, :, ls], qh) for k_ref in (k0_ref, k1_ref)]

    coming = scores(0)
    halves = []
    for i in range(2 * pairs):
        s0, s1 = coming
        if i + 1 < 2 * pairs:
            coming = scores(i + 1)
        top = jnp.maximum(col_max(s0), col_max(s1))
        vs = slice(i * HEAD, (i + 1) * HEAD)
        e0 = jnp.exp2((s0 - top) * SOFTMAX_MUL)
        o = jnp.dot(v0_ref[0, vs, :], e0.astype(BF), preferred_element_type=F32)
        total = col_sum(e0)
        e1 = jnp.exp2((s1 - top) * SOFTMAX_MUL)
        o += jnp.dot(v1_ref[0, vs, :], e1.astype(BF), preferred_element_type=F32)
        total += col_sum(e1)
        halves.append(o / total)
        if i % 2:
            p = i // 2
            o_ref[0, :, p * LANES:(p + 1) * LANES] = jnp.transpose(jnp.concatenate(halves, axis=0)).astype(BF)
            halves = []


def attn_call(q, k0, k1, v0, v1, pairs=5):
    lat, tok, chan = q.shape
    width = LANES * pairs
    qs = pl.BlockSpec((1, tok, width), lambda b, h: (b, 0, h))
    vs = pl.BlockSpec((1, width, tok), lambda b, h: (b, h, 0))
    return pl.pallas_call(
        functools.partial(attn_kernel, pairs=pairs), grid=(lat, chan // width), in_specs=[qs, qs, qs, vs, vs], out_specs=qs,
        out_shape=like(q.shape), compiler_params=params(60),
        cost_estimate=cost(8 * lat * tok * tok * chan, 12 * lat * tok * chan), name="attn")(q, k0, k1, v0, v1)


def context_kernel(ctx_ref, w_ref, k_ref, v_ref):
    for l in range(ctx_ref.shape[0]):
        k_ref[0, l] = dot_nt(ctx_ref[l, 0:CTX_ROWS, :], w_ref[0, 0]).astype(BF)
        v_ref[0, l] = dot_nt(w_ref[0, 1], ctx_ref[l]).astype(BF)


def context_call(ctx, ckv_t):
    lat, padded, depth = ctx.shape
    layers, _, chan, _ = ckv_t.shape
    return pl.pallas_call(
        context_kernel, grid=(layers,),
        in_specs=[whole(ctx), major((1, 2, chan, depth))],
        out_specs=[major((1, lat, CTX_ROWS, chan)), major((1, lat, chan, padded))],
        out_shape=[like((layers, lat, CTX_ROWS, chan)), like((layers, lat, chan, padded))],
        compiler_params=params(60), cost_estimate=cost(4 * layers * lat * padded * depth * chan, 4 * layers * depth * chan), name="context")(ctx, ckv_t)


def post_kernel(att_ref, u_ref, wo_ref, ab_ref, ln_ref, wq_ref, kc_ref, vc_ref, wc_ref, out_ref, q_s, o_s, *, layer, ctx_len):
    tok, chan = u_ref.shape[1:]
    u = dot(att_ref[0], wo_ref[0, 0]) + u_ref[0].astype(F32) + row_of(ab_ref, layer, 0)
    u = u.astype(BF)
    out_ref[0] = u
    n = layer_norm(u.astype(F32), *affine(ln_ref, layer, 1))
    q_s[...] = dot_nt(n, wq_ref[0]).astype(BF)
    def scores(p):
        ls = at_lanes(p)
        kc = kc_ref[0, 0, :, ls]
        lane = lax.broadcasted_iota(jnp.int32, kc.shape, 1)
        zero = jnp.zeros_like(kc)
        both = jnp.concatenate([jnp.where(lane < HEAD, kc, zero), jnp.where(lane >= HEAD, kc, zero)], axis=0)
        return dot_nt(both, q_s[:, ls])

    pairs = chan // LANES
    coming = scores(0)
    for p in range(pairs):
        s = coming
        if p + 1 < pairs:
            coming = scores(p + 1)
        exps, sums = [], []
        for h in range(2):
            sh = s[at_lanes(h, CTX_ROWS)]
            valid = lax.broadcasted_iota(jnp.int32, sh.shape, 0) < ctx_len
            sh = jnp.where(valid, sh, -jnp.inf)
            e = jnp.exp2((sh - col_max(sh)) * SOFTMAX_MUL)
            sums.append(col_sum(e))
            exps += [e.astype(BF), jnp.zeros((LANES - CTX_ROWS, tok), BF)]
        vc = vc_ref[0, 0, at_lanes(p), :]
        row = lax.broadcasted_iota(jnp.int32, vc.shape, 0)
        zero = jnp.zeros_like(vc)
        vb = jnp.concatenate([jnp.where(row < HEAD, vc, zero), jnp.where(row >= HEAD, vc, zero)], axis=1)
        o = dot(vb, jnp.concatenate(exps, axis=0))
        o = jnp.concatenate([o[:HEAD] / sums[0], o[HEAD:] / sums[1]], axis=0)
        o_s[:, at_lanes(p)] = jnp.transpose(o).astype(BF)
    y = dot(o_s[...], wc_ref[0, 0]) + out_ref[0].astype(F32) + row_of(ab_ref, layer, 1)
    out_ref[0] = y.astype(BF)


def post_call(att, u, attn_out, attn_b, ln_par, cq_t, kc, vc, layer, ctx_len):
    lat, tok, chan = u.shape
    row = major((1, tok, chan))
    mat = lambda i: fixed((1, 1, chan, chan), layer, i)
    ctx_spec = lambda a: pl.BlockSpec((1, 1) + a.shape[2:], lambda b: (layer, b, 0, 0))
    return pl.pallas_call(
        functools.partial(post_kernel, layer=layer, ctx_len=ctx_len), grid=(lat,),
        in_specs=[row, row, mat(0), whole(attn_b), whole(ln_par), fixed((1, chan, chan), layer), ctx_spec(kc), ctx_spec(vc), mat(1)],
        out_specs=row, out_shape=like(u.shape),
        scratch_shapes=[pltpu.VMEM((tok, chan), BF)] * 2,
        compiler_params=params(60), cost_estimate=cost(6 * lat * tok * chan * chan, 6 * chan * chan), name="post")(
            att, u, attn_out, attn_b, ln_par, cq_t, kc, vc, attn_out)


def ffn_kernel(u_ref, ln_ref, w1a_ref, w1b_ref, b1a_ref, b1b_ref, w2_ref, b2_ref, out_ref, n_s, acc_s, *, layer, chunk):
    step = pl.program_id(0)
    tokens = u_ref.shape[0]

    @pl.when(step == 0)
    def _():
        def body(r, carry):
            rr = pl.ds(pl.multiple_of(r * LANES, LANES), LANES)
            x = u_ref[rr, :].astype(F32)
            n_s[rr, :] = layer_norm(x, *affine(ln_ref, layer, 2))
            acc_s[rr, :] = x + row_of(b2_ref, layer)
            return carry

        lax.fori_loop(0, tokens // LANES, body, 0)

    for m in range(tokens // chunk):
        rr = slice(m * chunk, (m + 1) * chunk)
        n = n_s[rr, :]
        p2 = dot(n, w1b_ref[0]) + row_of(b1b_ref, layer)
        p1 = dot(n, w1a_ref[0]) + row_of(b1a_ref, layer)
        half = 0.5 * p2
        gated = (p1 * (half + half * lax.erf(p2 * math.sqrt(0.5)))).astype(BF)
        acc_s[rr, :] += dot(gated, w2_ref[0])

    @pl.when(step == pl.num_programs(0) - 1)
    def _():
        out_ref[...] = acc_s[...].astype(BF)


def ffn_call(u, ln_par, w1, b1, w2, b2, layer, ft=512, chunk=512):
    tokens, chan = u.shape
    width = w2.shape[1]
    n = width // ft
    layers = w1.shape[0]
    return pl.pallas_call(
        functools.partial(ffn_kernel, layer=layer, chunk=chunk), grid=(n,),
        in_specs=[whole(u), whole(ln_par), minor((1, chan, ft), layer), pl.BlockSpec((1, chan, ft), lambda i: (layer, 0, i + n)),
                  minor((layers, ft)), pl.BlockSpec((layers, ft), lambda i: (0, i + n)),
                  pl.BlockSpec((1, ft, chan), lambda i: (layer, i, 0)), whole(b2)],
        out_specs=whole(u), out_shape=like(u.shape),
        scratch_shapes=[pltpu.VMEM(u.shape, BF), pltpu.VMEM(u.shape, F32)],
        compiler_params=params(60), cost_estimate=cost(6 * tokens * chan * width, 6 * chan * width), name="ffn")(u, ln_par, w1, w1, b1, b1, w2, b2)


def leave_kernel(core_ref, u_ref, w_ref, pb_ref, h_ref, out_ref, sum_ref, edge_ref):
    sums, squares = [], []
    core = core_ref[0]
    tok = u_ref.shape[1]
    for l in range(u_ref.shape[0]):
        y = dot(u_ref[l], w_ref[0]) + row_of(pb_ref, 1) + h_ref[l].astype(F32)
        y = y.astype(BF)
        out_ref[l] = y
        edge_ref[l] = jnp.where(core == 0, y[tok - LANES:], y[:LANES])
        y = y.astype(F32)
        sums.append(col_sum(y))
        squares.append(col_sum(y * y))
    sum_ref[...] = place_rows(sums, squares, 0)


def leave_call(core, u, proj_w, proj_b, h, nt=256):
    lat, tok, chan = u.shape
    return pl.pallas_call(
        leave_kernel,
        grid_spec=pltpu.PrefetchScalarGridSpec(
            num_scalar_prefetch=1, grid=(chan // nt,),
            in_specs=[whole(u), minor((1, chan, nt), 1), minor((2, nt)), minor((lat, tok, nt))],
            out_specs=[minor((lat, tok, nt)), minor((SUM_ROWS, nt)), minor((lat, LANES, nt))]),
        out_shape=[like(u.shape), like((SUM_ROWS, chan), F32), like((lat, LANES, chan))],
        compiler_params=params(60), cost_estimate=cost(2 * lat * tok * chan * chan, 2 * chan * chan), name="leave")(core, u, proj_w, proj_b, h)


SWAP = pairs_of('01 10 23 32')


def device_block(latents, time_emb, context, res_norm, res_conv_w, res_conv_b, res_temb_w, res_temb_b, tr_norm, proj_w, proj_b, ln_par, self_qkv, cross_q, cross_kv, attn_out, attn_b, ff_in_w, ff_in_b, ff_out_w, ff_out_b):
    index = lax.axis_index('sp')
    chip, core = index // 2, index % 2
    core_vec = jnp.reshape(core, (1,)).astype(jnp.int32)
    count, rows_n, cols, chan = latents.shape
    lat = count // 2
    tok = 2 * rows_n * cols
    ctx_len = context.shape[1]
    where = jnp.reshape(index, (1,)).astype(jnp.int32)
    flat = latents.reshape(count, rows_n * cols, chan)
    arrived = []
    for l in (2, 0, 1):
        low, high = flat[l:l + 1], flat[lat + l:lat + l + 1]
        first = lax.ppermute(jnp.where(core == 0, high, low), 'sp', pairs_of('02 10 23 31'))
        second = lax.ppermute(jnp.where(chip == 0, high, low), 'sp', pairs_of('12 21'))
        arrived.append((first, second))

    temb = lax.dynamic_slice(time_emb, (chip * lat, 0), (lat, chan))
    temb = jax.nn.silu(temb.astype(F32)).astype(BF)
    tembs = [dot(temb, res_temb_w[r]) + res_temb_b[r] for r in range(2)]
    ctx = lax.dynamic_slice(context, (chip * lat, 0, 0), (lat,) + context.shape[1:])
    ctx = jnp.pad(ctx, ((0, 0), (0, LANES - ctx_len), (0, 0)))
    ckv_t = jnp.moveaxis(cross_kv, 2, -1).reshape(cross_kv.shape[:2] + (chan, -1))
    kc, vc = context_call(ctx, ckv_t)
    qkv_t = jnp.moveaxis(self_qkv, 2, -1).reshape(self_qkv.shape[:2] + (chan, chan))
    cq_t = jnp.moveaxis(cross_q, 1, -1).reshape(-1, chan, chan)
    attn_w = attn_out.reshape(attn_b.shape[:2] + (chan, chan))
    conv_w = res_conv_w.reshape(-1, KERNEL, KERNEL * chan, chan)

    swap = lambda a: lax.ppermute(a, 'sp', SWAP)
    early, kc, vc, tembs = lax.optimization_barrier((arrived[0], kc, vc, tembs))
    v, own, edge = gather_call(where, flat, early[:1], early[1:], 2)
    into = conv_call(core_vec, v, swap(edge), own, swap(own), res_norm, res_conv_b, conv_w, 0, 0, temb=tembs[0], base=2, lat=1)
    late, v, into = lax.optimization_barrier((arrived[1:], v, into))
    v, own, edge = gather_call(where, flat, [a[0] for a in late], [a[1] for a in late], 0, into=v)
    t, sums_t, edge = conv_call(core_vec, v, swap(edge), own, swap(own), res_norm, res_conv_b, conv_w, 0, 0, temb=tembs[0], into=into, base=0, lat=2)
    h, sums_h, _ = conv_call(core_vec, t, swap(edge), sums_t, swap(sums_t), res_norm, res_conv_b, conv_w, 0, 1, res=v)
    u, n, k = enter_call(h, sums_h, swap(sums_h), tr_norm, proj_w, proj_b, ln_par, qkv_t)
    for layer in range(2):
        if layer:
            n, k = key_call(u, ln_par, qkv_t, layer)
        k_far = swap(k)
        vals = linear_call(value_kernel, n, qkv_t, layer, 2, (chan, tok), "values")
        vals_far = swap(vals)
        q = linear_call(query_kernel, n, qkv_t, layer, 0, (tok, chan), "queries")
        att = attn_call(q, k, k_far, vals, vals_far)
        u = post_call(att, u, attn_w, attn_b, ln_par, cq_t, kc, vc, layer, ctx_len)
        u = ffn_call(u.reshape(lat * tok, chan), ln_par, ff_in_w, ff_in_b, ff_out_w, ff_out_b, layer).reshape(lat, tok, chan)
    h, sums_h, edge = leave_call(core_vec, u, proj_w, proj_b, h)
    t, sums_t, edge = conv_call(core_vec, h, swap(edge), sums_h, swap(sums_h), res_norm, res_conv_b, conv_w, 1, 0, temb=tembs[1])
    edge, peer = swap(edge), swap(sums_t)
    lows, highs = [], []
    for l in range(lat):
        out = conv_call(core_vec, t, edge, sums_t, peer, res_norm, res_conv_b, conv_w, 1, 1, res=h, base=l, lat=1, want_sums=False)
        top, bottom = out[:, :tok // 2], out[:, tok // 2:]
        first = lax.ppermute(jnp.where(chip == 0, bottom, top), 'sp', pairs_of('20 01 32 13'))
        second = lax.ppermute(jnp.where(core == 0, bottom, top), 'sp', pairs_of('21 12'))
        third = jnp.where(index == 0, top, jnp.where(index == 3, bottom, second))
        lows.append(jnp.where(core == 0, third, first))
        highs.append(jnp.where(core == 0, first, third))
    return jnp.concatenate(lows + highs, axis=0).reshape(latents.shape)


def solution(mesh):
    row_spec = P('dp', 'sp')
    part_spec = P('dp')
    in_specs = (row_spec, part_spec, part_spec) + (P(),) * 18
    return jax.shard_map(device_block, mesh=mesh, in_specs=in_specs, out_specs=row_spec, check_vma=False)
```

time: 2100 us -> 717 us (0.34)
  matrix products: 922 us -> 6.18 us
  Pallas kernels: 0 us -> 629 us
  local copies, waits for them, and re-layouts: 499 us -> 8.23 us
  blocking collectives: 214 us -> 0 us
  other arithmetic: 208 us -> 12.6 us
  waiting for transfers between devices: 208 us -> 29.2 us
    dot_general x50 -> x2, matrix products: 689 us -> 6.18 us  [dot(): return jnp.dot(left, right, preferred_element_type=F32)]
    pallas_call x0 -> x23, Pallas kernels: none -> 629 us  [the longest x7 238 us: conv_call(): pl.pallas_call(body, grid_spec=pltpu.PrefetchScalarGridSpec(num_scalar_pr...]
    conv_general_dilated x4 -> x0, matrix products: 232 us -> none  [conv_rows(): lax.conv_general_dilated(padded, kernel, (1, 1), ((0, 0), (1, 1)), dimens...]
    all_to_all x3 -> x0, waiting for transfers between devices: 201 us -> none  [the longest x1 129 us: transformer_local(): qkv_heads = lax.all_to_all(qkv_loc, 'sp', 3, 2, tiled=True)]
    all_to_all x1 -> x0, blocking collectives: 133 us -> none  [transformer_local(): qkv_heads = lax.all_to_all(qkv_loc, 'sp', 3, 2, tiled=True)]
    reduce_sum x40 -> x0, other arithmetic: 110 us -> none  [the longest x18 75.2 us: attend_block(): row_sum = row_exp.sum(axis=-1)]
    psum x5 -> x0, blocking collectives: 81.8 us -> none  [group_norm_sp(): total_sums = lax.psum(local_sums, 'sp')]
    convert_element_type x18 -> x0, local copies, waits for them, and re-layouts: 80.4 us -> none  [the longest x14 44.4 us: resnet_local(): jax.nn.silu(group_norm_sp(hidden, res_norm[res_index, 1, 0], res_norm[res...]
  transfers between devices with their start and end apart: 11 -> 27, of which waited for: 6 -> 9; matrix products, arithmetic and copies ran while one was open for 3% -> 2% of each run, Pallas kernels for 0% -> 13%
where the time goes in v1:
time: 717 us; the launch traced here: 711 us
  Pallas kernels  629 us (88%)
  waiting for transfers between devices  29.2 us (4%)
  starting transfers between devices  26 us (4%)
  other arithmetic  12.6 us (2%)
  local copies, waits for them, and re-layouts  8.23 us (1%)
    pallas_call x7, Pallas kernels, conv_call(): pl.pallas_call(body, grid_spec=pltpu.PrefetchScalarGridSpec(num_scalar_pr...  238 us
    pallas_call x2, Pallas kernels, ffn_call(): pl.pallas_call(functools.partial(ffn_kernel, layer=layer, chunk=chunk), g...  150 us
    pallas_call x2, Pallas kernels, attn_call(): pl.pallas_call(functools.partial(attn_kernel, pairs=pairs), grid=(lat, ch...  84.5 us
    pallas_call x2, Pallas kernels, post_call(): pl.pallas_call(functools.partial(post_kernel, layer=layer, ctx_len=ctx_le...  58.5 us
    pallas_call x4, Pallas kernels, linear_call(): pl.pallas_call(kernel, grid=(lat,), in_specs=[major((1, tok, chan)), fixe...  36.5 us
    pallas_call x1, Pallas kernels, enter_call(): pl.pallas_call(enter_kernel, grid=(lat,), in_specs=[row, whole(own), whol...  20.3 us
    ppermute x15, waiting for transfers between devices, device_block(): swap = lambda a: lax.ppermute(a, 'sp', SWAP)  14.4 us
  transfers between devices with their start and end apart: 27, of which 9 were waited for; matrix products, arithmetic and copies ran while one was open for 2% of the time, Pallas kernels for 13%

profile of v1, /device:TPU:0, one launch (start us, length us, event | category | flops | bytes accessed | tf_op | source)
XLA Modules:
  0.0 711.4 jit_solution(4632802857307530832)
XLA Ops:
  0.0 3.5 broadcast_select_fusion.3
  3.5 3.2 collective-permute-start.4
  9.3 3.1 fusion.6.rest_0_
  12.4 3.1 fusion.9.rest_0_
  15.5 12.5 %context.1 = (bf16[2,3,80,1280]{3,2,1,0:T(8,128)(2,1)}, bf16[2,3,1280,128]{3,2,1,0:T(8,128)(2,1)}) custom-call(bf16[3,128,1024]{2,1,0:T(8,128)(2,1)} %pad.4.ctx_ref, bf16[2,2,1280,1024]{3,2,1,0:T(8,128)(2,1)} %bitcast.53), custom_call_target="tpu_custom_call" | custom-call | flops 4026531840 | bytes 10485760 | tf_op jit(solution)/shard_map/context/pallas_call | solution.py:394
  28.1 2.6 gather.2
  37.7 21.2 %conv.7 = (bf16[3,512,1280]{2,1,0:T(8,128)(2,1)}, f32[8,1280]{1,0:T(8,128)}, bf16[3,128,1280]{2,1,0:T(8,128)(2,1)}) custom-call(s32[1]{0:T(128)} %bitcast.core_ref, bf16[3,512,1280]{2,1,0:T(8,128)(2,1)} %get-tuple-element.61.v_ref.rest_4_, bf16[1,128,1280]{2,1,0:T(8,128)(2,1)} %copy-done.9, f32[8,1280]{1,0:T(8,128)} %get-tuple-element.52.own_ref, ...), custom_call_target="tpu_custom_call" | custom-call | flops 15099494400 | bytes 29491200 | tf_op jit(solution)/shard_map/conv/pallas_call | solution.py:227
  59.5 3.7 gather.3
  63.2 2.8 collective-permute-start.8
  68.6 39.1 %conv.8 = (bf16[3,512,1280]{2,1,0:T(8,128)(2,1)}, f32[8,1280]{1,0:T(8,128)}, bf16[3,128,1280]{2,1,0:T(8,128)(2,1)}) custom-call(s32[1]{0:T(128)} %bitcast.core_ref, bf16[3,512,1280]{2,1,0:T(8,128)(2,1)} %get-tuple-element.62.v_ref.rest_1_, bf16[2,128,1280]{2,1,0:T(8,128)(2,1)} %copy-done.7, ...), custom_call_target="tpu_custom_call", output_to_operand_aliasing={{0}: (9, {}), {2}: (10, {})} | custom-call | flops 30198988800 | bytes 29491200 | tf_op jit(solution)/shard_map/conv/pallas_call | solution.py:227
  111.4 57.0 %conv.9 = (bf16[3,512,1280]{2,1,0:T(8,128)(2,1)}, f32[8,1280]{1,0:T(8,128)}, bf16[3,128,1280]{2,1,0:T(8,128)(2,1)}) custom-call(s32[1]{0:T(128)} %bitcast.core_ref, bf16[3,512,1280]{2,1,0:T(8,128)(2,1)} %get-tuple-element.68.v_ref, bf16[3,128,1280]{2,1,0:T(8,128)(2,1)} %copy-done.14, f32[8,1280]{1,0:T(8,128)} %get-tuple-element.70.own_ref, ...), custom_call_target="tpu_custom_call" | custom-call | flops 45298483200 | bytes 29491200 | tf_op jit(solution)/shard_map/conv/pallas_call | solution.py:227
  170.4 20.3 %enter.1 = (bf16[3,512,1280]{2,1,0:T(8,128)(2,1)}, bf16[3,512,1280]{2,1,0:T(8,128)(2,1)}, bf16[3,512,1280]{2,1,0:T(8,128)(2,1)}) custom-call(bf16[3,512,1280]{2,1,0:T(8,128)(2,1)} %get-tuple-element.71.h_ref, f32[8,1280]{1,0:T(8,128)} %get-tuple-element.72.own_ref, f32[8,1280]{1,0:T(8,128)} %copy-done.18, f32[2,1280]{1,0:T(2,128)} %norm_ref.11, ...), custom_call_target="tpu_custom_call" | custom-call | flops 10066329600 | bytes 6553600 | tf_op jit(solution)/shard_map/enter/pallas_call | solution.py:302
  190.7 9.1 %values.2.v0_ref = bf16[3,1280,512]{2,1,0:T(8,128)(2,1)} custom-call(bf16[3,512,1280]{2,1,0:T(8,128)(2,1)} %get-tuple-element.73.n_ref, bf16[2,3,1280,1280]{3,2,1,0:T(8,128)(2,1)} %bitcast.36), custom_call_target="tpu_custom_call" | custom-call | flops 209715200 | bytes 3276800 | tf_op jit(solution)/shard_map/values/pallas_call | solution.py:337
  200.3 9.1 %queries.2.q_ref = bf16[3,512,1280]{2,1,0:T(8,128)(2,1)} custom-call(bf16[3,512,1280]{2,1,0:T(8,128)(2,1)} %get-tuple-element.73.n_ref, bf16[2,3,1280,1280]{3,2,1,0:T(8,128)(2,1)} %bitcast.37), custom_call_target="tpu_custom_call" | custom-call | flops 209715200 | bytes 3276800 | tf_op jit(solution)/shard_map/queries/pallas_call | solution.py:337
  209.4 2.7 collective-permute-done.13.k1_ref
  212.2 42.3 %attn.2.att_ref = bf16[3,512,1280]{2,1,0:T(8,128)(2,1)} custom-call(bf16[3,512,1280]{2,1,0:T(8,128)(2,1)} %queries.2.q_ref, bf16[3,512,1280]{2,1,0:T(8,128)(2,1)} %get-tuple-element.74.k0_ref, bf16[3,512,1280]{2,1,0:T(8,128)(2,1)} %collective-permute-done.13.k1_ref, bf16[3,1280,512]{2,1,0:T(8,128)(2,1)} %values.2.v0_ref, ...), custom_call_target="tpu_custom_call" | custom-call | flops 8053063680 | bytes 23592960 | tf_op jit(solution)/shard_map/attn/pallas_call | solution.py:379
  254.5 29.2 %post.2 = bf16[3,512,1280]{2,1,0:T(8,128)(2,1)} custom-call(bf16[3,512,1280]{2,1,0:T(8,128)(2,1)} %attn.2.att_ref, bf16[3,512,1280]{2,1,0:T(8,128)(2,1)} %get-tuple-element.75.u_ref, bf16[2,2,1280,1280]{3,2,1,0:T(8,128)(2,1)} %bitcast.49, f32[2,2,1280]{2,1,0:T(2,128)} %ab_ref.3, f32[2,3,2,1280]{3,2,1,0:T(2,128)} %ln_ref.11, bf16[2,1280,1280]{2,1,0:T(8,128)(2,1)} %bitcast.54, ...), custom_call_target="tpu_custom_call" | custom-call | flops 15099494400 | bytes 9830400 | tf_op jit(solution)/shard_map/post/pallas_call | solution.py:447
  283.7 75.0 %ffn.2 = bf16[1536,1280]{1,0:T(8,128)(2,1)} custom-call(bf16[1536,1280]{1,0:T(8,128)(2,1)} %bitcast.58, f32[2,3,2,1280]{3,2,1,0:T(2,128)} %ln_ref.11, bf16[2,1280,10240]{2,1,0:T(8,128)(2,1)} %w1b_ref.3, bf16[2,1280,10240]{2,1,0:T(8,128)(2,1)} %w1b_ref.3, f32[2,10240]{1,0:T(2,128)} %b1b_ref.3, f32[2,10240]{1,0:T(2,128)} %b1b_ref.3, ...), custom_call_target="tpu_custom_call" | custom-call | flops 60397977600 | bytes 39321600 | tf_op jit(solution)/shard_map/ffn/pallas_call | solution.py:490
  358.7 11.0 %keys.1 = (bf16[3,512,1280]{2,1,0:T(8,128)(2,1)}, bf16[3,512,1280]{2,1,0:T(8,128)(2,1)}) custom-call(bf16[3,512,1280]{2,1,0:T(8,128)(2,1)} %bitcast.43, f32[2,3,2,1280]{3,2,1,0:T(2,128)} %ln_ref.11, bf16[2,3,1280,1280]{3,2,1,0:T(8,128)(2,1)} %bitcast.38), custom_call_target="tpu_custom_call" | custom-call | flops 5033164800 | bytes 3276800 | tf_op jit(solution)/shard_map/keys/pallas_call | solution.py:320
  369.7 9.1 %values.3.v0_ref = bf16[3,1280,512]{2,1,0:T(8,128)(2,1)} custom-call(bf16[3,512,1280]{2,1,0:T(8,128)(2,1)} %get-tuple-element.78.n_ref, bf16[2,3,1280,1280]{3,2,1,0:T(8,128)(2,1)} %bitcast.39), custom_call_target="tpu_custom_call" | custom-call | flops 209715200 | bytes 3276800 | tf_op jit(solution)/shard_map/values/pallas_call | solution.py:337
  379.3 9.1 %queries.3.q_ref = bf16[3,512,1280]{2,1,0:T(8,128)(2,1)} custom-call(bf16[3,512,1280]{2,1,0:T(8,128)(2,1)} %get-tuple-element.78.n_ref, bf16[2,3,1280,1280]{3,2,1,0:T(8,128)(2,1)} %bitcast.40), custom_call_target="tpu_custom_call" | custom-call | flops 209715200 | bytes 3276800 | tf_op jit(solution)/shard_map/queries/pallas_call | solution.py:337
  388.5 2.7 collective-permute-done.15.k1_ref
  391.2 42.2 %attn.3.att_ref = bf16[3,512,1280]{2,1,0:T(8,128)(2,1)} custom-call(bf16[3,512,1280]{2,1,0:T(8,128)(2,1)} %queries.3.q_ref, bf16[3,512,1280]{2,1,0:T(8,128)(2,1)} %get-tuple-element.79.k0_ref, bf16[3,512,1280]{2,1,0:T(8,128)(2,1)} %collective-permute-done.15.k1_ref, bf16[3,1280,512]{2,1,0:T(8,128)(2,1)} %values.3.v0_ref, ...), custom_call_target="tpu_custom_call" | custom-call | flops 8053063680 | bytes 23592960 | tf_op jit(solution)/shard_map/attn/pallas_call | solution.py:379
  433.4 29.4 %post.3 = bf16[3,512,1280]{2,1,0:T(8,128)(2,1)} custom-call(bf16[3,512,1280]{2,1,0:T(8,128)(2,1)} %attn.3.att_ref, bf16[3,512,1280]{2,1,0:T(8,128)(2,1)} %bitcast.44, bf16[2,2,1280,1280]{3,2,1,0:T(8,128)(2,1)} %bitcast.51, f32[2,2,1280]{2,1,0:T(2,128)} %ab_ref.3, f32[2,3,2,1280]{3,2,1,0:T(2,128)} %ln_ref.11, bf16[2,1280,1280]{2,1,0:T(8,128)(2,1)} %bitcast.55, ...), custom_call_target="tpu_custom_call" | custom-call | flops 15099494400 | bytes 9830400 | tf_op jit(solution)/shard_map/post/pallas_call | solution.py:447
  462.8 75.0 %ffn.3 = bf16[1536,1280]{1,0:T(8,128)(2,1)} custom-call(bf16[1536,1280]{1,0:T(8,128)(2,1)} %bitcast.57, f32[2,3,2,1280]{3,2,1,0:T(2,128)} %ln_ref.11, bf16[2,1280,10240]{2,1,0:T(8,128)(2,1)} %w1b_ref.3, bf16[2,1280,10240]{2,1,0:T(8,128)(2,1)} %w1b_ref.3, f32[2,10240]{1,0:T(2,128)} %b1b_ref.3, f32[2,10240]{1,0:T(2,128)} %b1b_ref.3, ...), custom_call_target="tpu_custom_call" | custom-call | flops 60397977600 | bytes 39321600 | tf_op jit(solution)/shard_map/ffn/pallas_call | solution.py:490
  537.8 11.1 %leave.1 = (bf16[3,512,1280]{2,1,0:T(8,128)(2,1)}, f32[8,1280]{1,0:T(8,128)}, bf16[3,128,1280]{2,1,0:T(8,128)(2,1)}) custom-call(s32[1]{0:T(128)} %bitcast.core_ref, bf16[3,512,1280]{2,1,0:T(8,128)(2,1)} %bitcast.56, bf16[2,1280,1280]{2,1,0:T(8,128)(2,1)} %w_ref.1, f32[2,1280]{1,0:T(2,128)} %pb_ref.3, bf16[3,512,1280]{2,1,0:T(8,128)(2,1)} %get-tuple-element.71.h_ref), custom_call_target="tpu_custom_call" | custom-call | flops 5033164800 | bytes 3276800 | tf_op jit(solution)/shard_map/leave/pallas_call | solution.py:517
  552.5 56.6 %conv.10 = (bf16[3,512,1280]{2,1,0:T(8,128)(2,1)}, f32[8,1280]{1,0:T(8,128)}, bf16[3,128,1280]{2,1,0:T(8,128)(2,1)}) custom-call(s32[1]{0:T(128)} %bitcast.core_ref, bf16[3,512,1280]{2,1,0:T(8,128)(2,1)} %get-tuple-element.80.v_ref.rest_1_, bf16[3,128,1280]{2,1,0:T(8,128)(2,1)} %copy-done.15, f32[8,1280]{1,0:T(8,128)} %get-tuple-element.82.own_ref, ...), custom_call_target="tpu_custom_call" | custom-call | flops 45298483200 | bytes 29491200 | tf_op jit(solution)/shard_map/conv/pallas_call | solution.py:227
  612.8 21.5 %conv.12 = bf16[1,512,1280]{2,1,0:T(8,128)(2,1)} custom-call(s32[1]{0:T(128)} %bitcast.core_ref, bf16[3,512,1280]{2,1,0:T(8,128)(2,1)} %get-tuple-element.84.v_ref, bf16[3,128,1280]{2,1,0:T(8,128)(2,1)} %copy-done.5, f32[8,1280]{1,0:T(8,128)} %get-tuple-element.86.own_ref, f32[8,1280]{1,0:T(8,128)} %copy-done.8, f32[2,2,2,1280]{3,2,1,0:T(2,128)} %norm_ref.15, ...), custom_call_target="tpu_custom_call" | custom-call | flops 15099494400 | bytes 29491200 | tf_op jit(solution)/shard_map/conv/pallas_call | solution.py:227
  637.5 2.7 collective-permute-start.24
  640.2 21.2 %conv.11 = bf16[1,512,1280]{2,1,0:T(8,128)(2,1)} custom-call(s32[1]{0:T(128)} %bitcast.core_ref, bf16[3,512,1280]{2,1,0:T(8,128)(2,1)} %get-tuple-element.84.v_ref, bf16[3,128,1280]{2,1,0:T(8,128)(2,1)} %copy-done.5, f32[8,1280]{1,0:T(8,128)} %get-tuple-element.86.own_ref, f32[8,1280]{1,0:T(8,128)} %copy-done.8, f32[2,2,2,1280]{3,2,1,0:T(2,128)} %norm_ref.15, ...), custom_call_target="tpu_custom_call" | custom-call | flops 15099494400 | bytes 29491200 | tf_op jit(solution)/shard_map/conv/pallas_call | solution.py:227
  666.5 21.2 %conv.13 = bf16[1,512,1280]{2,1,0:T(8,128)(2,1)} custom-call(s32[1]{0:T(128)} %bitcast.core_ref, bf16[3,512,1280]{2,1,0:T(8,128)(2,1)} %get-tuple-element.84.v_ref, bf16[3,128,1280]{2,1,0:T(8,128)(2,1)} %copy-done.5, f32[8,1280]{1,0:T(8,128)} %get-tuple-element.86.own_ref, f32[8,1280]{1,0:T(8,128)} %copy-done.8, f32[2,2,2,1280]{3,2,1,0:T(2,128)} %norm_ref.15, ...), custom_call_target="tpu_custom_call" | custom-call | flops 15099494400 | bytes 29491200 | tf_op jit(solution)/shard_map/conv/pallas_call | solution.py:227
  694.3 14.1 %collective-permute-done.26 = bf16[1,256,1280]{2,1,0:T(8,128)(2,1)S(1)} collective-permute-done((bf16[1,256,1280]{2,1,0:T(8,128)(2,1)S(1)}, bf16[1,256,1280]{2,1,0:T(8,128)(2,1)S(1)}, u32[]{:S(2)}, u32[]{:S(2)}) %collective-permute-start.26) | collective-permute-done | bytes 655392 | tf_op jit(solution)/shard_map/ppermute | solution.py:585
  (100 shorter events, 44.2 us)
Async XLA Ops:
  0.0 8.3 %copy-start = (bf16[6,77,1024]{2,1,0:T(8,128)(2,1)S(1)}, bf16[6,77,1024]{2,1,0:T(8,128)(2,1)}, u32[]{:S(2)}) copy-start(bf16[6,77,1024]{2,1,0:T(8,128)(2,1)} %param.23) | copy-start | bytes 2838532
  0.0 8.3 %copy-start.13 = (f32[2,1280]{1,0:T(2,128)S(1)}, f32[2,1280]{1,0:T(2,128)}, u32[]{:S(2)}) copy-start(f32[2,1280]{1,0:T(2,128)} %param.28) | copy-start | bytes 30724
  0.0 9.3 %copy-start.19 = (bf16[6,1280]{1,0:T(8,128)(2,1)S(1)}, bf16[6,1280]{1,0:T(8,128)(2,1)}, u32[]{:S(2)}) copy-start(bf16[6,1280]{1,0:T(8,128)(2,1)} %param.22) | copy-start | bytes 46084
  3.5 24.5 %collective-permute-start.4 = (bf16[1,256,1280]{2,1,0:T(8,128)(2,1)}, bf16[1,256,1280]{2,1,0:T(8,128)(2,1)}, u32[]{:S(2)}, u32[]{:S(2)}) collective-permute-start(bf16[1,256,1280]{2,1,0:T(8,128)(2,1)} %bitcast.7), channel_id=1, source_target_pairs={{0,2},{1,0},{2,3},{3,1},{4,6},{5,4},{6,7},{7,5},{8,10},{9,8},{10,1... | collective-permute-start | bytes 1966088 | tf_op jit(solution)/shard_map/ppermute | solution.py:543
  6.8 21.3 %collective-permute-start.5 = (bf16[1,256,1280]{2,1,0:T(8,128)(2,1)}, bf16[1,256,1280]{2,1,0:T(8,128)(2,1)}, u32[]{:S(2)}, u32[]{:S(2)}) collective-permute-start(bf16[1,256,1280]{2,1,0:T(8,128)(2,1)} %bitcast.8), channel_id=1, source_target_pairs={{1,2},{2,1},{5,6},{6,5},{9,10},{10,9},{13,14},{14,13}} | collective-permute-start | bytes 1966088 | tf_op jit(solution)/shard_map/ppermute | solution.py:544
  30.7 6.3 collective-permute-start.6
  31.3 4.1 collective-permute-start.7
  31.3 27.6 %collective-permute-start = (bf16[1,256,1280]{2,1,0:T(8,128)(2,1)S(1)}, bf16[1,256,1280]{2,1,0:T(8,128)(2,1)}, u32[]{:S(2)}, u32[]{:S(2)}) collective-permute-start(bf16[1,256,1280]{2,1,0:T(8,128)(2,1)S(1)} %bitcast.48), channel_id=1, source_target_pairs={{0,2},{1,0},{2,3},{3,1},{4,6},{5,4},{6,7},{7,5},{8,10},{9,8},{10,1... | collective-permute-start | bytes 1966088 | tf_op jit(solution)/shard_map/ppermute | solution.py:543
  31.7 27.2 %collective-permute-start.1 = (bf16[1,256,1280]{2,1,0:T(8,128)(2,1)S(1)}, bf16[1,256,1280]{2,1,0:T(8,128)(2,1)}, u32[]{:S(2)}, u32[]{:S(2)}) collective-permute-start(bf16[1,256,1280]{2,1,0:T(8,128)(2,1)S(1)} %bitcast.47), channel_id=1, source_target_pairs={{1,2},{2,1},{5,6},{6,5},{9,10},{10,9},{13,14},{14,13}} | collective-permute-start | bytes 1966088 | tf_op jit(solution)/shard_map/ppermute | solution.py:544
  33.2 26.3 %collective-permute-start.2 = (bf16[1,256,1280]{2,1,0:T(8,128)(2,1)S(1)}, bf16[1,256,1280]{2,1,0:T(8,128)(2,1)}, u32[]{:S(2)}, u32[]{:S(2)}) collective-permute-start(bf16[1,256,1280]{2,1,0:T(8,128)(2,1)S(1)} %bitcast.46), channel_id=1, source_target_pairs={{0,2},{1,0},{2,3},{3,1},{4,6},{5,4},{6,7},{7,5},{8,10},{9,8},{10,1... | collective-permute-start | bytes 1966088 | tf_op jit(solution)/shard_map/ppermute | solution.py:543
  35.3 24.2 %collective-permute-start.3 = (bf16[1,256,1280]{2,1,0:T(8,128)(2,1)S(1)}, bf16[1,256,1280]{2,1,0:T(8,128)(2,1)}, u32[]{:S(2)}, u32[]{:S(2)}) collective-permute-start(bf16[1,256,1280]{2,1,0:T(8,128)(2,1)S(1)} %bitcast.45), channel_id=1, source_target_pairs={{1,2},{2,1},{5,6},{6,5},{9,10},{10,9},{13,14},{14,13}} | collective-permute-start | bytes 1966088 | tf_op jit(solution)/shard_map/ppermute | solution.py:544
  63.2 4.5 collective-permute-start.8
  66.0 1.8 collective-permute-start.9
  107.7 2.7 collective-permute-start.10
  108.1 2.3 collective-permute-start.11
  168.5 1.3 collective-permute-start.12
  199.8 9.7 %collective-permute-start.14 = (bf16[3,1280,512]{2,1,0:T(8,128)(2,1)}, bf16[3,1280,512]{2,1,0:T(8,128)(2,1)}, u32[]{:S(2)}, u32[]{:S(2)}) collective-permute-start(bf16[3,1280,512]{2,1,0:T(8,128)(2,1)} %values.2.v0_ref), channel_id=1, source_target_pairs={{0,1},{1,0},{2,3},{3,2},{4,5},{5,4},{6,7},{7,6},{8,9},{9,8},{10,11... | collective-permute-start | bytes 11796488 | tf_op jit(solution)/shard_map/ppermute | solution.py:559
  200.1 12.0 %collective-permute-start.13 = (bf16[3,512,1280]{2,1,0:T(8,128)(2,1)}, bf16[3,512,1280]{2,1,0:T(8,128)(2,1)}, u32[]{:S(2)}, u32[]{:S(2)}) collective-permute-start(bf16[3,512,1280]{2,1,0:T(8,128)(2,1)} %get-tuple-element.74.k0_ref), channel_id=1, source_target_pairs={{0,1},{1,0},{2,3},{3,2},{4,5},{5,4},{6,7},{7,6},{8,9},{9,8},{10,11... | collective-permute-start | bytes 11796488 | tf_op jit(solution)/shard_map/ppermute | solution.py:559
  378.8 9.7 %collective-permute-start.16 = (bf16[3,1280,512]{2,1,0:T(8,128)(2,1)}, bf16[3,1280,512]{2,1,0:T(8,128)(2,1)}, u32[]{:S(2)}, u32[]{:S(2)}) collective-permute-start(bf16[3,1280,512]{2,1,0:T(8,128)(2,1)} %values.3.v0_ref), channel_id=1, source_target_pairs={{0,1},{1,0},{2,3},{3,2},{4,5},{5,4},{6,7},{7,6},{8,9},{9,8},{10,11... | collective-permute-start | bytes 11796488 | tf_op jit(solution)/shard_map/ppermute | solution.py:559
  379.1 12.0 %collective-permute-start.15 = (bf16[3,512,1280]{2,1,0:T(8,128)(2,1)}, bf16[3,512,1280]{2,1,0:T(8,128)(2,1)}, u32[]{:S(2)}, u32[]{:S(2)}) collective-permute-start(bf16[3,512,1280]{2,1,0:T(8,128)(2,1)} %get-tuple-element.79.k0_ref), channel_id=1, source_target_pairs={{0,1},{1,0},{2,3},{3,2},{4,5},{5,4},{6,7},{7,6},{8,9},{9,8},{10,11... | collective-permute-start | bytes 11796488 | tf_op jit(solution)/shard_map/ppermute | solution.py:559
  548.9 2.6 collective-permute-start.17
  549.2 2.3 collective-permute-start.18
  609.1 2.7 collective-permute-start.19
  609.5 2.3 collective-permute-start.20
  636.8 57.1 %collective-permute-start.23 = (bf16[1,256,1280]{2,1,0:T(8,128)(2,1)}, bf16[1,256,1280]{2,1,0:T(8,128)(2,1)S(1)}, u32[]{:S(2)}, u32[]{:S(2)}) collective-permute-start(bf16[1,256,1280]{2,1,0:T(8,128)(2,1)} %get-tuple-element.103), channel_id=1, source_target_pairs={{2,1},{1,2},{6,5},{5,6},{10,9},{9,10},{14,13},{13,14}} | collective-permute-start | bytes 1966088 | tf_op jit(solution)/shard_map/ppermute | solution.py:586
  637.5 56.4 %collective-permute-start.24 = (bf16[1,256,1280]{2,1,0:T(8,128)(2,1)}, bf16[1,256,1280]{2,1,0:T(8,128)(2,1)S(1)}, u32[]{:S(2)}, u32[]{:S(2)}) collective-permute-start(bf16[1,256,1280]{2,1,0:T(8,128)(2,1)} %get-tuple-element.104), channel_id=1, source_target_pairs={{2,0},{0,1},{3,2},{1,3},{6,4},{4,5},{7,6},{5,7},{10,8},{8,9},{11,1... | collective-permute-start | bytes 1966088 | tf_op jit(solution)/shard_map/ppermute | solution.py:585
  663.9 26.0 %collective-permute-start.21 = (bf16[1,256,1280]{2,1,0:T(8,128)(2,1)}, bf16[1,256,1280]{2,1,0:T(8,128)(2,1)}, u32[]{:S(2)}, u32[]{:S(2)}) collective-permute-start(bf16[1,256,1280]{2,1,0:T(8,128)(2,1)} %get-tuple-element.105), channel_id=1, source_target_pairs={{2,1},{1,2},{6,5},{5,6},{10,9},{9,10},{14,13},{13,14}} | collective-permute-start | bytes 1966088 | tf_op jit(solution)/shard_map/ppermute | solution.py:586
  665.4 27.0 %copy-start.4 = (bf16[1,512,1280]{2,1,0:T(8,128)(2,1)S(1)}, bf16[1,512,1280]{2,1,0:T(8,128)(2,1)}, u32[]{:S(2)}) copy-start(bf16[1,512,1280]{2,1,0:T(8,128)(2,1)} %conv.11) | copy-start | bytes 3932164
  665.4 27.0 %collective-permute-start.22 = (bf16[1,256,1280]{2,1,0:T(8,128)(2,1)}, bf16[1,256,1280]{2,1,0:T(8,128)(2,1)S(1)}, u32[]{:S(2)}, u32[]{:S(2)}) collective-permute-start(bf16[1,256,1280]{2,1,0:T(8,128)(2,1)} %get-tuple-element.106), channel_id=1, source_target_pairs={{2,0},{0,1},{3,2},{1,3},{6,4},{4,5},{7,6},{5,7},{10,8},{8,9},{11,1... | collective-permute-start | bytes 1966088 | tf_op jit(solution)/shard_map/ppermute | solution.py:585
  689.2 5.1 collective-permute-start.25
  689.9 18.5 %copy-start.3 = (bf16[1,512,1280]{2,1,0:T(8,128)(2,1)S(1)}, bf16[1,512,1280]{2,1,0:T(8,128)(2,1)}, u32[]{:S(2)}) copy-start(bf16[1,512,1280]{2,1,0:T(8,128)(2,1)} %conv.13) | copy-start | bytes 3932164
  689.9 18.5 %collective-permute-start.26 = (bf16[1,256,1280]{2,1,0:T(8,128)(2,1)S(1)}, bf16[1,256,1280]{2,1,0:T(8,128)(2,1)S(1)}, u32[]{:S(2)}, u32[]{:S(2)}) collective-permute-start(bf16[1,256,1280]{2,1,0:T(8,128)(2,1)S(1)} %get-tuple-element.102), channel_id=1, source_target_pairs={{2,0},{0,1},{3,2},{1,3},{6,4},{4,5},{7,6},{5,7},{10,8},{8,9},{11,1... | collective-permute-start | bytes 1966088 | tf_op jit(solution)/shard_map/ppermute | solution.py:585
  (15 other events, 23.5 us)

commit v2 on v1

--- a/solution.py
+++ b/solution.py
@@ -18,6 +18,7 @@
 LATENTS = 3
 KERNEL = 3
 WIDE = 256
+CHUNKS = 2
 SUM_ROWS = 8
 CTX_ROWS = 80
 SOFTMAX_MUL = math.log2(math.e) / math.sqrt(HEAD)
@@ -125,10 +126,10 @@
         _, _, before_ref = rest[:3]
         rest = rest[3:]
     out_ref = rest.pop(0)
-    sum_ref, edge_ref = rest if want_sums else (None, None)
+    sum_ref, edge_ref = rest if want_sums else (rest[0], None)
     lat, tok, chan = v_ref.shape
     rows = tok // LANES
-    core = core_ref[0]
+    core, chip = core_ref[0] % 2, core_ref[0] // 2
     step, steps = pl.program_id(0), pl.num_programs(0)
     nt = out_ref.shape[-1]
 
@@ -182,12 +183,16 @@
         if has_res:
             acc += res_ref[l].astype(F32)
         out = acc.astype(BF)
-        out_ref[l] = out
         if want_sums:
+            out_ref[l] = out
             edge_ref[l] = jnp.where(core == 0, out[tok - LANES:], out[:LANES])
             out = out.astype(F32)
             sums.append(col_sum(out))
             squares.append(col_sum(out * out))
+        else:
+            half = tok // 2
+            out_ref[l] = jnp.where(chip == 0, out[half:], out[:half])
+            sum_ref[l] = jnp.where(chip == 0, out[:half], out[half:])
     if want_sums:
         placed = place_rows(sums, squares, base)
         sum_ref[...] = placed + before_ref[...] if has_into else placed
@@ -214,15 +219,17 @@
         args.append(res)
     aliases = {}
     held = LATENTS if want_sums else lat
-    out = like((held, tok, chan))
+    out = like((held, tok if want_sums else tok // 2, chan))
     if into is not None:
         aliases = {len(args) + 1: 0, len(args) + 2: 2}
         specs += [any_space(), any_space(), minor((SUM_ROWS, nt))]
         args += [into[0], into[2], into[1]]
-    out_specs, out_shape = [tile(out, tok)], [out]
+    out_specs, out_shape = [tile(out, out.shape[1])], [out]
     if want_sums:
         out_specs += [minor((SUM_ROWS, nt)), tile(out, LANES)]
         out_shape += [like((SUM_ROWS, chan), F32), like((held, LANES, chan))]
+    else:
+        out_specs, out_shape = out_specs * 2, out_shape * 2
     body = functools.partial(conv_kernel, res_i=res_i, conv_i=conv_i, eps=1e-5, base=base, has_temb=temb is not None, has_res=res is not None, has_into=into is not None, want_sums=want_sums)
     outs = pl.pallas_call(
         body,
@@ -231,23 +238,21 @@
             scratch_shapes=[pltpu.VMEM((lat, tok + 2 * LANES, KERNEL * chan), BF), pltpu.VMEM((2, KERNEL, KERNEL * chan, nt), BF), pltpu.SemaphoreType.DMA((2,))]),
         out_shape=out_shape, compiler_params=params(60), input_output_aliases=aliases,
         cost_estimate=cost(18 * lat * tok * chan * chan, 18 * chan * chan), name="conv")(core, *args)
-    return outs if want_sums else outs[0]
-
-
-def gather_kernel(where_ref, own_ref, *rest, base, lat, has_into):
-    firsts, seconds = rest[:lat], rest[lat:2 * lat]
+    return outs
+
+
+def gather_kernel(where_ref, *rest, base, lat, has_into):
+    parts = rest[:2 * lat]
     v_ref, sum_ref, edge_ref = rest[2 * lat + has_into:]
     index = where_ref[0]
     chip, core = index // 2, index % 2
-    half = own_ref.shape[1]
-    mine = jnp.logical_or(index == 0, index == 3)
     sums, squares = [], []
     for l in range(lat):
-        third = jnp.where(mine, own_ref[l], seconds[l][0])
-        first = firsts[l][0]
-        top = jnp.where(chip == 0, third, first)
-        bottom = jnp.where(chip == 0, first, third)
-        v_ref[l, 0:half] = top
+        first, second = parts[2 * l][0], parts[2 * l + 1][0]
+        half = first.shape[0]
+        top = jnp.where(chip == 0, second, first)
+        bottom = jnp.where(chip == 0, first, second)
+        v_ref[l, :half] = top
         v_ref[l, half:] = bottom
         edge_ref[l] = jnp.where(core == 0, bottom[half - LANES:], top[:LANES])
         top, bottom = top.astype(F32), bottom.astype(F32)
@@ -256,13 +261,13 @@
     sum_ref[...] = place_rows(sums, squares, base)
 
 
-def gather_call(where, flat, firsts, seconds, base, into=None):
-    lat = len(firsts)
-    half, chan = flat.shape[1:]
+def gather_call(where, first, second, base, into=None):
+    lat, half, chan = first.shape
     nt = 640
-    part = minor((1, half, nt))
-    specs = [pl.BlockSpec((pl.Element(lat), pl.Element(half), pl.Element(nt)), lambda n, w: (w[0] // 2 * LATENTS + base, 0, n * nt))] + [part] * (2 * lat)
-    args = [flat, *firsts, *seconds]
+    specs, args = [], []
+    for l in range(lat):
+        specs += [minor((1, half, nt), l)] * 2
+        args += [first, second]
     aliases = {}
     if into is not None:
         specs.append(any_space())
@@ -288,12 +293,16 @@
         scale_s[:LATENTS] = inv * row_of(norm_ref, 0)
 
     mean, scale = mean_s[pl.ds(step, 1), :], scale_s[pl.ds(step, 1), :]
-    normed = ((h_ref[0].astype(F32) - mean) * scale + row_of(norm_ref, 1)).astype(BF)
-    u = (dot(normed, pw_ref[0]) + row_of(pb_ref, 0)).astype(BF)
-    u_ref[0] = u
-    n = layer_norm(u.astype(F32), *affine(ln_ref, 0, 0))
-    n_ref[0] = n
-    k_ref[0] = dot_nt(n, wk_ref[0, 0]).astype(BF)
+    chunks = [at_lanes(i, h_ref.shape[1] // CHUNKS) for i in range(CHUNKS)]
+    tokens = []
+    for rr in chunks:
+        normed = ((h_ref[0, rr].astype(F32) - mean) * scale + row_of(norm_ref, 1)).astype(BF)
+        tokens.append((dot(normed, pw_ref[0]) + row_of(pb_ref, 0)).astype(BF))
+    for rr, u in zip(chunks, tokens):
+        u_ref[0, rr] = u
+        n = layer_norm(u.astype(F32), *affine(ln_ref, 0, 0))
+        n_ref[0, rr] = n
+        k_ref[0, rr] = dot_nt(n, wk_ref[0, 0]).astype(BF)
 
 
 def enter_call(h, own, peer, tr_norm, proj_w, proj_b, ln_par, qkv_t):
@@ -309,9 +318,11 @@
 
 
 def key_kernel(u_ref, ln_ref, wk_ref, n_ref, k_ref, *, layer):
-    n = layer_norm(u_ref[0].astype(F32), *affine(ln_ref, layer, 0))
-    n_ref[0] = n
-    k_ref[0] = dot_nt(n, wk_ref[0, 0]).astype(BF)
+    for i in range(CHUNKS):
+        rr = at_lanes(i, u_ref.shape[1] // CHUNKS)
+        n = layer_norm(u_ref[0, rr].astype(F32), *affine(ln_ref, layer, 0))
+        n_ref[0, rr] = n
+        k_ref[0, rr] = dot_nt(n, wk_ref[0, 0]).astype(BF)
 
 
 def key_call(u, ln_par, qkv_t, layer):
@@ -383,9 +394,13 @@
 
 
 def context_kernel(ctx_ref, w_ref, k_ref, v_ref):
-    for l in range(ctx_ref.shape[0]):
-        k_ref[0, l] = dot_nt(ctx_ref[l, 0:CTX_ROWS, :], w_ref[0, 0]).astype(BF)
-        v_ref[0, l] = dot_nt(w_ref[0, 1], ctx_ref[l]).astype(BF)
+    lat, padded, depth = ctx_ref.shape
+    tokens = ctx_ref[...].reshape(lat * padded, depth)
+    keys = dot_nt(tokens, w_ref[0, 0]).astype(BF)
+    values = dot_nt(w_ref[0, 1], tokens).astype(BF)
+    for l in range(lat):
+        k_ref[0, l] = keys[l * padded:l * padded + CTX_ROWS]
+        v_ref[0, l] = values[:, at_lanes(l, padded)]
 
 
 def context_call(ctx, ckv_t):
@@ -399,20 +414,15 @@
         compiler_params=params(60), cost_estimate=cost(4 * layers * lat * padded * depth * chan, 4 * layers * depth * chan), name="context")(ctx, ckv_t)
 
 
-def post_kernel(att_ref, u_ref, wo_ref, ab_ref, ln_ref, wq_ref, kc_ref, vc_ref, wc_ref, out_ref, q_s, o_s, *, layer, ctx_len):
-    tok, chan = u_ref.shape[1:]
-    u = dot(att_ref[0], wo_ref[0, 0]) + u_ref[0].astype(F32) + row_of(ab_ref, layer, 0)
-    u = u.astype(BF)
-    out_ref[0] = u
-    n = layer_norm(u.astype(F32), *affine(ln_ref, layer, 1))
-    q_s[...] = dot_nt(n, wq_ref[0]).astype(BF)
+def cross_attend(q_s, kc_ref, vc_ref, o_s, ctx_len):
+    tok, chan = q_s.shape
+
     def scores(p):
-        ls = at_lanes(p)
-        kc = kc_ref[0, 0, :, ls]
+        kc = kc_ref[0, 0, :, at_lanes(p)]
         lane = lax.broadcasted_iota(jnp.int32, kc.shape, 1)
         zero = jnp.zeros_like(kc)
         both = jnp.concatenate([jnp.where(lane < HEAD, kc, zero), jnp.where(lane >= HEAD, kc, zero)], axis=0)
-        return dot_nt(both, q_s[:, ls])
+        return dot_nt(both, q_s[:, at_lanes(p)])
 
     pairs = chan // LANES
     coming = scores(0)
@@ -435,66 +445,61 @@
         o = dot(vb, jnp.concatenate(exps, axis=0))
         o = jnp.concatenate([o[:HEAD] / sums[0], o[HEAD:] / sums[1]], axis=0)
         o_s[:, at_lanes(p)] = jnp.transpose(o).astype(BF)
-    y = dot(o_s[...], wc_ref[0, 0]) + out_ref[0].astype(F32) + row_of(ab_ref, layer, 1)
-    out_ref[0] = y.astype(BF)
-
-
-def post_call(att, u, attn_out, attn_b, ln_par, cq_t, kc, vc, layer, ctx_len):
-    lat, tok, chan = u.shape
-    row = major((1, tok, chan))
-    mat = lambda i: fixed((1, 1, chan, chan), layer, i)
-    ctx_spec = lambda a: pl.BlockSpec((1, 1) + a.shape[2:], lambda b: (layer, b, 0, 0))
-    return pl.pallas_call(
-        functools.partial(post_kernel, layer=layer, ctx_len=ctx_len), grid=(lat,),
-        in_specs=[row, row, mat(0), whole(attn_b), whole(ln_par), fixed((1, chan, chan), layer), ctx_spec(kc), ctx_spec(vc), mat(1)],
-        out_specs=row, out_shape=like(u.shape),
-        scratch_shapes=[pltpu.VMEM((tok, chan), BF)] * 2,
-        compiler_params=params(60), cost_estimate=cost(6 * lat * tok * chan * chan, 6 * chan * chan), name="post")(
-            att, u, attn_out, attn_b, ln_par, cq_t, kc, vc, attn_out)
-
-
-def ffn_kernel(u_ref, ln_ref, w1a_ref, w1b_ref, b1a_ref, b1b_ref, w2_ref, b2_ref, out_ref, n_s, acc_s, *, layer, chunk):
+
+
+def rest_kernel(att_ref, u_ref, wo_ref, ab_ref, ln_ref, wq_ref, kc_ref, vc_ref, wc_ref, w1a_ref, w1b_ref, b1a_ref, b1b_ref, w2_ref, b2_ref, out_ref, q_s, o_s, u_s, n_s, acc_s, *, layer, ctx_len, lat, chunk):
     step = pl.program_id(0)
-    tokens = u_ref.shape[0]
-
-    @pl.when(step == 0)
+    tok = u_ref.shape[1]
+    chunks = [at_lanes(i, tok // CHUNKS) for i in range(CHUNKS)]
+
+    @pl.when(step < lat)
     def _():
-        def body(r, carry):
-            rr = pl.ds(pl.multiple_of(r * LANES, LANES), LANES)
-            x = u_ref[rr, :].astype(F32)
-            n_s[rr, :] = layer_norm(x, *affine(ln_ref, layer, 2))
-            acc_s[rr, :] = x + row_of(b2_ref, layer)
-            return carry
-
-        lax.fori_loop(0, tokens // LANES, body, 0)
-
-    for m in range(tokens // chunk):
-        rr = slice(m * chunk, (m + 1) * chunk)
-        n = n_s[rr, :]
-        p2 = dot(n, w1b_ref[0]) + row_of(b1b_ref, layer)
-        p1 = dot(n, w1a_ref[0]) + row_of(b1a_ref, layer)
-        half = 0.5 * p2
-        gated = (p1 * (half + half * lax.erf(p2 * math.sqrt(0.5)))).astype(BF)
-        acc_s[rr, :] += dot(gated, w2_ref[0])
+        for rr in chunks:
+            u_s[rr] = (dot(att_ref[0, rr], wo_ref[0, 0]) + u_ref[0, rr].astype(F32) + row_of(ab_ref, layer, 0)).astype(BF)
+        for rr in chunks:
+            q_s[rr] = dot_nt(layer_norm(u_s[rr].astype(F32), *affine(ln_ref, layer, 1)), wq_ref[0]).astype(BF)
+        cross_attend(q_s, kc_ref, vc_ref, o_s, ctx_len)
+        for rr in chunks:
+            y = (dot(o_s[rr], wc_ref[0, 0]) + u_s[rr].astype(F32) + row_of(ab_ref, layer, 1)).astype(BF).astype(F32)
+            rows = pl.ds(pl.multiple_of(step * tok + rr.start, LANES), rr.stop - rr.start)
+            n_s[rows] = layer_norm(y, *affine(ln_ref, layer, 2))
+            acc_s[rows] = y + row_of(b2_ref, layer)
+
+    @pl.when(step >= lat)
+    def _():
+        for m in range(n_s.shape[0] // chunk):
+            rr = at_lanes(m, chunk)
+            n = n_s[rr]
+            p2 = dot(n, w1b_ref[0]) + row_of(b1b_ref, layer)
+            p1 = dot(n, w1a_ref[0]) + row_of(b1a_ref, layer)
+            half = 0.5 * p2
+            gated = (p1 * (half + half * lax.erf(p2 * math.sqrt(0.5)))).astype(BF)
+            acc_s[rr] += dot(gated, w2_ref[0])
 
     @pl.when(step == pl.num_programs(0) - 1)
     def _():
         out_ref[...] = acc_s[...].astype(BF)
 
 
-def ffn_call(u, ln_par, w1, b1, w2, b2, layer, ft=512, chunk=512):
-    tokens, chan = u.shape
+def rest_call(att, u, attn_out, attn_b, ln_par, cq_t, kc, vc, w1, b1, w2, b2, layer, ctx_len, ft=512, chunk=512):
+    lat, tok, chan = u.shape
     width = w2.shape[1]
     n = width // ft
-    layers = w1.shape[0]
-    return pl.pallas_call(
-        functools.partial(ffn_kernel, layer=layer, chunk=chunk), grid=(n,),
-        in_specs=[whole(u), whole(ln_par), minor((1, chan, ft), layer), pl.BlockSpec((1, chan, ft), lambda i: (layer, 0, i + n)),
-                  minor((layers, ft)), pl.BlockSpec((layers, ft), lambda i: (0, i + n)),
-                  pl.BlockSpec((1, ft, chan), lambda i: (layer, i, 0)), whole(b2)],
-        out_specs=whole(u), out_shape=like(u.shape),
-        scratch_shapes=[pltpu.VMEM(u.shape, BF), pltpu.VMEM(u.shape, F32)],
-        compiler_params=params(60), cost_estimate=cost(6 * tokens * chan * width, 6 * chan * width), name="ffn")(u, ln_par, w1, w1, b1, b1, w2, b2)
+    row = pl.BlockSpec((1, tok, chan), lambda i: (jnp.minimum(i, lat - 1), 0, 0))
+    ctx_spec = lambda a: pl.BlockSpec((1, 1) + a.shape[2:], lambda i: (layer, jnp.minimum(i, lat - 1), 0, 0))
+    mat = lambda i: fixed((1, 1, chan, chan), layer, i)
+    part = lambda i: jnp.maximum(i - lat, 0)
+    flat = (lat * tok, chan)
+    return pl.pallas_call(
+        functools.partial(rest_kernel, layer=layer, ctx_len=ctx_len, lat=lat, chunk=chunk), grid=(lat + n,),
+        in_specs=[row, row, mat(0), whole(attn_b), whole(ln_par), fixed((1, chan, chan), layer), ctx_spec(kc), ctx_spec(vc), mat(1),
+                  pl.BlockSpec((1, chan, ft), lambda i: (layer, 0, part(i))), pl.BlockSpec((1, chan, ft), lambda i: (layer, 0, part(i) + n)),
+                  pl.BlockSpec((w1.shape[0], ft), lambda i: (0, part(i))), pl.BlockSpec((w1.shape[0], ft), lambda i: (0, part(i) + n)),
+                  pl.BlockSpec((1, ft, chan), lambda i: (layer, part(i), 0)), whole(b2)],
+        out_specs=fixed(flat), out_shape=like(flat),
+        scratch_shapes=[pltpu.VMEM((tok, chan), BF)] * 3 + [pltpu.VMEM(flat, BF), pltpu.VMEM(flat, F32)],
+        compiler_params=params(62), cost_estimate=cost(6 * lat * tok * chan * (chan + width), 6 * chan * (chan + width)), name="rest")(
+            att, u, attn_out, attn_b, ln_par, cq_t, kc, vc, attn_out, w1, w1, b1, b1, w2, b2)
 
 
 def leave_kernel(core_ref, u_ref, w_ref, pb_ref, h_ref, out_ref, sum_ref, edge_ref):
@@ -537,12 +542,13 @@
     ctx_len = context.shape[1]
     where = jnp.reshape(index, (1,)).astype(jnp.int32)
     flat = latents.reshape(count, rows_n * cols, chan)
-    arrived = []
-    for l in (2, 0, 1):
-        low, high = flat[l:l + 1], flat[lat + l:lat + l + 1]
-        first = lax.ppermute(jnp.where(core == 0, high, low), 'sp', pairs_of('02 10 23 31'))
-        second = lax.ppermute(jnp.where(chip == 0, high, low), 'sp', pairs_of('12 21'))
-        arrived.append((first, second))
+    halves = flat.reshape(2, lat, rows_n * cols, chan)
+    going, staying = lax.dynamic_index_in_dim(halves, 1 - core, keepdims=False), lax.dynamic_index_in_dim(halves, core, keepdims=False)
+
+    def spread(part):
+        return lax.ppermute(going[part], 'sp', pairs_of('02 10 23 31')), lax.ppermute(staying[part], 'sp', pairs_of('12 21 00 33'))
+
+    early, late = spread(slice(lat - 1, lat)), spread(slice(0, lat - 1))
 
     temb = lax.dynamic_slice(time_emb, (chip * lat, 0), (lat, chan))
     temb = jax.nn.silu(temb.astype(F32)).astype(BF)
@@ -557,13 +563,13 @@
     conv_w = res_conv_w.reshape(-1, KERNEL, KERNEL * chan, chan)
 
     swap = lambda a: lax.ppermute(a, 'sp', SWAP)
-    early, kc, vc, tembs = lax.optimization_barrier((arrived[0], kc, vc, tembs))
-    v, own, edge = gather_call(where, flat, early[:1], early[1:], 2)
-    into = conv_call(core_vec, v, swap(edge), own, swap(own), res_norm, res_conv_b, conv_w, 0, 0, temb=tembs[0], base=2, lat=1)
-    late, v, into = lax.optimization_barrier((arrived[1:], v, into))
-    v, own, edge = gather_call(where, flat, [a[0] for a in late], [a[1] for a in late], 0, into=v)
-    t, sums_t, edge = conv_call(core_vec, v, swap(edge), own, swap(own), res_norm, res_conv_b, conv_w, 0, 0, temb=tembs[0], into=into, base=0, lat=2)
-    h, sums_h, _ = conv_call(core_vec, t, swap(edge), sums_t, swap(sums_t), res_norm, res_conv_b, conv_w, 0, 1, res=v)
+    early, kc, vc, tembs = lax.optimization_barrier((early, kc, vc, tembs))
+    v, own, edge = gather_call(where, *early, 2)
+    into = conv_call(where, v, swap(edge), own, swap(own), res_norm, res_conv_b, conv_w, 0, 0, temb=tembs[0], base=2, lat=1)
+    late, v, into = lax.optimization_barrier((late, v, into))
+    v, own, edge = gather_call(where, *late, 0, into=v)
+    t, sums_t, edge = conv_call(where, v, swap(edge), own, swap(own), res_norm, res_conv_b, conv_w, 0, 0, temb=tembs[0], into=into, base=0, lat=2)
+    h, sums_h, _ = conv_call(where, t, swap(edge), sums_t, swap(sums_t), res_norm, res_conv_b, conv_w, 0, 1, res=v)
     u, n, k = enter_call(h, sums_h, swap(sums_h), tr_norm, proj_w, proj_b, ln_par, qkv_t)
     for layer in range(2):
         if layer:
@@ -573,18 +579,15 @@
         vals_far = swap(vals)
         q = linear_call(query_kernel, n, qkv_t, layer, 0, (tok, chan), "queries")
         att = attn_call(q, k, k_far, vals, vals_far)
-        u = post_call(att, u, attn_w, attn_b, ln_par, cq_t, kc, vc, layer, ctx_len)
-        u = ffn_call(u.reshape(lat * tok, chan), ln_par, ff_in_w, ff_in_b, ff_out_w, ff_out_b, layer).reshape(lat, tok, chan)
+        u = rest_call(att, u, attn_w, attn_b, ln_par, cq_t, kc, vc, ff_in_w, ff_in_b, ff_out_w, ff_out_b, layer, ctx_len).reshape(lat, tok, chan)
     h, sums_h, edge = leave_call(core_vec, u, proj_w, proj_b, h)
-    t, sums_t, edge = conv_call(core_vec, h, swap(edge), sums_h, swap(sums_h), res_norm, res_conv_b, conv_w, 1, 0, temb=tembs[1])
+    t, sums_t, edge = conv_call(where, h, swap(edge), sums_h, swap(sums_h), res_norm, res_conv_b, conv_w, 1, 0, temb=tembs[1])
     edge, peer = swap(edge), swap(sums_t)
     lows, highs = [], []
     for l in range(lat):
-        out = conv_call(core_vec, t, edge, sums_t, peer, res_norm, res_conv_b, conv_w, 1, 1, res=h, base=l, lat=1, want_sums=False)
-        top, bottom = out[:, :tok // 2], out[:, tok // 2:]
-        first = lax.ppermute(jnp.where(chip == 0, bottom, top), 'sp', pairs_of('20 01 32 13'))
-        second = lax.ppermute(jnp.where(core == 0, bottom, top), 'sp', pairs_of('21 12'))
-        third = jnp.where(index == 0, top, jnp.where(index == 3, bottom, second))
+        going, staying = conv_call(where, t, edge, sums_t, peer, res_norm, res_conv_b, conv_w, 1, 1, res=h, base=l, lat=1, want_sums=False)
+        first = lax.ppermute(going, 'sp', pairs_of('20 01 32 13'))
+        third = lax.ppermute(staying, 'sp', pairs_of('21 12 00 33'))
         lows.append(jnp.where(core == 0, third, first))
         highs.append(jnp.where(core == 0, first, third))
     return jnp.concatenate(lows + highs, axis=0).reshape(latents.shape)

time: 717 us -> 693 us (0.967)
  Pallas kernels: 629 us -> 607 us
  other arithmetic: 12.6 us -> 0.93 us
  local copies, waits for them, and re-layouts: 8.23 us -> 17.3 us
    pallas_call x4 -> x2, Pallas kernels: 209 us -> 196 us  [rest_call(): pl.pallas_call(functools.partial(rest_kernel, layer=layer, ctx_len=ctx_le...]
    select_n x4 -> x0, other arithmetic: 9.95 us -> none  [the longest x3 6.41 us: device_block(): jnp.where(core == 0, bottom, top)]
    ppermute x12 -> x10, waiting for transfers between devices: 14.7 us -> 19.3 us  [the longest x3 15.5 us: device_block(): first = lax.ppermute(going, 'sp', pairs_of('20 01 32 13'))]
    ppermute x12 -> x10, starting transfers between devices: 19.6 us -> 15.7 us  [the longest x3 5.24 us: device_block(): third = lax.ppermute(staying, 'sp', pairs_of('21 12 00 33'))]
  transfers between devices with their start and end apart: 27 -> 25, of which waited for: 9 -> 9; matrix products, arithmetic and copies ran while one was open for 2% -> 2% of each run, Pallas kernels for 13% -> 13%
where the time goes in v2:
time: 693 us; the launch traced here: 688 us
  Pallas kernels  607 us (88%)
  waiting for transfers between devices  33.7 us (5%)
  starting transfers between devices  22.5 us (3%)
  local copies, waits for them, and re-layouts  17.3 us (2%)
    pallas_call x7, Pallas kernels, conv_call(): pl.pallas_call(body, grid_spec=pltpu.PrefetchScalarGridSpec(num_scalar_pr...  238 us
    pallas_call x2, Pallas kernels, rest_call(): pl.pallas_call(functools.partial(rest_kernel, layer=layer, ctx_len=ctx_le...  196 us
    pallas_call x2, Pallas kernels, attn_call(): pl.pallas_call(functools.partial(attn_kernel, pairs=pairs), grid=(lat, ch...  83.8 us
    pallas_call x4, Pallas kernels, linear_call(): pl.pallas_call(kernel, grid=(lat,), in_specs=[major((1, tok, chan)), fixe...  36.5 us
    pallas_call x1, Pallas kernels, enter_call(): pl.pallas_call(enter_kernel, grid=(lat,), in_specs=[row, whole(own), whol...  17.1 us
    ppermute x3, waiting for transfers between devices, device_block(): first = lax.ppermute(going, 'sp', pairs_of('20 01 32 13'))  15.5 us
    ppermute x15, waiting for transfers between devices, device_block(): swap = lambda a: lax.ppermute(a, 'sp', SWAP)  14.5 us
  transfers between devices with their start and end apart: 25, of which 9 were waited for; matrix products, arithmetic and copies ran while one was open for 2% of the time, Pallas kernels for 13%

profile of v2, /device:TPU:0, one launch (start us, length us, event | category | flops | bytes accessed | tf_op | source)
XLA Modules:
  0.0 688.5 jit_solution(9803030866806349010)
XLA Ops:
  0.0 2.3 dynamic-slice_bitcast_fusion.2
  2.3 3.2 collective-permute-start.2
  8.1 3.1 fusion.6.rest_0_
  11.2 3.1 fusion.9.rest_0_
  14.3 8.9 %context.1 = (bf16[2,3,80,1280]{3,2,1,0:T(8,128)(2,1)}, bf16[2,3,1280,128]{3,2,1,0:T(8,128)(2,1)}) custom-call(bf16[3,128,1024]{2,1,0:T(8,128)(2,1)} %pad.4.ctx_ref, bf16[2,2,1280,1024]{3,2,1,0:T(8,128)(2,1)} %bitcast.49), custom_call_target="tpu_custom_call" | custom-call | flops 4026531840 | bytes 10485760 | tf_op jit(solution)/shard_map/context/pallas_call | solution.py:409
  24.3 2.4 gather.2
  28.0 3.4 dynamic-slice_bitcast_fusion
  31.8 2.1 collective-permute-start.1
  34.7 21.2 %conv.7 = (bf16[3,512,1280]{2,1,0:T(8,128)(2,1)}, f32[8,1280]{1,0:T(8,128)}, bf16[3,128,1280]{2,1,0:T(8,128)(2,1)}) custom-call(s32[1]{0:T(128)} %bitcast.where_ref.core_ref, bf16[3,512,1280]{2,1,0:T(8,128)(2,1)} %get-tuple-element.63.v_ref.rest_4_, bf16[1,128,1280]{2,1,0:T(8,128)(2,1)} %copy-done.9, f32[8,1280]{1,0:T(8,128)} %get-tuple-element.56.own_ref, ...), custom_call_target="tpu_custom_call" | custom-call | flops 15099494400 | bytes 29491200 | tf_op jit(solution)/shard_map/conv/pallas_call | solution.py:234
  55.9 3.7 collective-permute-done.rest_0_.rest_2_
  61.2 3.4 gather.3
  64.5 2.4 collective-permute-start.6
  69.6 39.1 %conv.8 = (bf16[3,512,1280]{2,1,0:T(8,128)(2,1)}, f32[8,1280]{1,0:T(8,128)}, bf16[3,128,1280]{2,1,0:T(8,128)(2,1)}) custom-call(s32[1]{0:T(128)} %bitcast.where_ref.core_ref, bf16[3,512,1280]{2,1,0:T(8,128)(2,1)} %get-tuple-element.64.v_ref.rest_1_, bf16[2,128,1280]{2,1,0:T(8,128)(2,1)} %copy-done.7, ...), custom_call_target="tpu_custom_call", output_to_operand_aliasing={{0}: (9, {}), {2}: (10, {})} | custom-call | flops 30198988800 | bytes 29491200 | tf_op jit(solution)/shard_map/conv/pallas_call | solution.py:234
  112.4 57.3 %conv.9 = (bf16[3,512,1280]{2,1,0:T(8,128)(2,1)}, f32[8,1280]{1,0:T(8,128)}, bf16[3,128,1280]{2,1,0:T(8,128)(2,1)}) custom-call(s32[1]{0:T(128)} %bitcast.where_ref.core_ref, bf16[3,512,1280]{2,1,0:T(8,128)(2,1)} %get-tuple-element.70.v_ref, bf16[3,128,1280]{2,1,0:T(8,128)(2,1)} %copy-done.13, f32[8,1280]{1,0:T(8,128)} %get-tuple-element.72.own_ref, ...), custom_call_target="tpu_custom_call" | custom-call | flops 45298483200 | bytes 29491200 | tf_op jit(solution)/shard_map/conv/pallas_call | solution.py:234
  171.6 17.1 %enter.1 = (bf16[3,512,1280]{2,1,0:T(8,128)(2,1)}, bf16[3,512,1280]{2,1,0:T(8,128)(2,1)}, bf16[3,512,1280]{2,1,0:T(8,128)(2,1)}) custom-call(bf16[3,512,1280]{2,1,0:T(8,128)(2,1)} %get-tuple-element.73.h_ref, f32[8,1280]{1,0:T(8,128)} %get-tuple-element.74.own_ref, f32[8,1280]{1,0:T(8,128)} %copy-done.17, f32[2,1280]{1,0:T(2,128)} %norm_ref.11, ...), custom_call_target="tpu_custom_call" | custom-call | flops 10066329600 | bytes 6553600 | tf_op jit(solution)/shard_map/enter/pallas_call | solution.py:311
  188.6 9.1 %values.2.v0_ref = bf16[3,1280,512]{2,1,0:T(8,128)(2,1)} custom-call(bf16[3,512,1280]{2,1,0:T(8,128)(2,1)} %get-tuple-element.75.n_ref, bf16[2,3,1280,1280]{3,2,1,0:T(8,128)(2,1)} %bitcast.36), custom_call_target="tpu_custom_call" | custom-call | flops 209715200 | bytes 3276800 | tf_op jit(solution)/shard_map/values/pallas_call | solution.py:348
  198.2 9.1 %queries.2.q_ref = bf16[3,512,1280]{2,1,0:T(8,128)(2,1)} custom-call(bf16[3,512,1280]{2,1,0:T(8,128)(2,1)} %get-tuple-element.75.n_ref, bf16[2,3,1280,1280]{3,2,1,0:T(8,128)(2,1)} %bitcast.37), custom_call_target="tpu_custom_call" | custom-call | flops 209715200 | bytes 3276800 | tf_op jit(solution)/shard_map/queries/pallas_call | solution.py:348
  207.3 2.8 collective-permute-done.11.k1_ref
  210.1 41.9 %attn.2.att_ref = bf16[3,512,1280]{2,1,0:T(8,128)(2,1)} custom-call(bf16[3,512,1280]{2,1,0:T(8,128)(2,1)} %queries.2.q_ref, bf16[3,512,1280]{2,1,0:T(8,128)(2,1)} %get-tuple-element.76.k0_ref, bf16[3,512,1280]{2,1,0:T(8,128)(2,1)} %collective-permute-done.11.k1_ref, bf16[3,1280,512]{2,1,0:T(8,128)(2,1)} %values.2.v0_ref, ...), custom_call_target="tpu_custom_call" | custom-call | flops 8053063680 | bytes 23592960 | tf_op jit(solution)/shard_map/attn/pallas_call | solution.py:390
  252.0 98.0 %rest.2 = bf16[1536,1280]{1,0:T(8,128)(2,1)} custom-call(bf16[3,512,1280]{2,1,0:T(8,128)(2,1)} %attn.2.att_ref, bf16[3,512,1280]{2,1,0:T(8,128)(2,1)} %get-tuple-element.77.u_ref, bf16[2,2,1280,1280]{3,2,1,0:T(8,128)(2,1)} %bitcast.45, f32[2,2,1280]{2,1,0:T(2,128)} %ab_ref.3, f32[2,3,2,1280]{3,2,1,0:T(2,128)} %ln_ref.7, bf16[2,1280,1280]{2,1,0:T(8,128)(2,1)} %bitcast.50, ...), custom_call_target="tpu_custom_call" | custom-call | flops 75497472000 | bytes 49152000 | tf_op jit(solution)/shard_map/rest/pallas_call | solution.py:493
  350.1 10.3 %keys.1 = (bf16[3,512,1280]{2,1,0:T(8,128)(2,1)}, bf16[3,512,1280]{2,1,0:T(8,128)(2,1)}) custom-call(bf16[3,512,1280]{2,1,0:T(8,128)(2,1)} %bitcast.43, f32[2,3,2,1280]{3,2,1,0:T(2,128)} %ln_ref.7, bf16[2,3,1280,1280]{3,2,1,0:T(8,128)(2,1)} %bitcast.38), custom_call_target="tpu_custom_call" | custom-call | flops 5033164800 | bytes 3276800 | tf_op jit(solution)/shard_map/keys/pallas_call | solution.py:331
  360.4 9.1 %values.3.v0_ref = bf16[3,1280,512]{2,1,0:T(8,128)(2,1)} custom-call(bf16[3,512,1280]{2,1,0:T(8,128)(2,1)} %get-tuple-element.80.n_ref, bf16[2,3,1280,1280]{3,2,1,0:T(8,128)(2,1)} %bitcast.39), custom_call_target="tpu_custom_call" | custom-call | flops 209715200 | bytes 3276800 | tf_op jit(solution)/shard_map/values/pallas_call | solution.py:348
  370.0 9.1 %queries.3.q_ref = bf16[3,512,1280]{2,1,0:T(8,128)(2,1)} custom-call(bf16[3,512,1280]{2,1,0:T(8,128)(2,1)} %get-tuple-element.80.n_ref, bf16[2,3,1280,1280]{3,2,1,0:T(8,128)(2,1)} %bitcast.40), custom_call_target="tpu_custom_call" | custom-call | flops 209715200 | bytes 3276800 | tf_op jit(solution)/shard_map/queries/pallas_call | solution.py:348
  379.2 2.7 collective-permute-done.13.k1_ref
  381.9 41.9 %attn.3.att_ref = bf16[3,512,1280]{2,1,0:T(8,128)(2,1)} custom-call(bf16[3,512,1280]{2,1,0:T(8,128)(2,1)} %queries.3.q_ref, bf16[3,512,1280]{2,1,0:T(8,128)(2,1)} %get-tuple-element.81.k0_ref, bf16[3,512,1280]{2,1,0:T(8,128)(2,1)} %collective-permute-done.13.k1_ref, bf16[3,1280,512]{2,1,0:T(8,128)(2,1)} %values.3.v0_ref, ...), custom_call_target="tpu_custom_call" | custom-call | flops 8053063680 | bytes 23592960 | tf_op jit(solution)/shard_map/attn/pallas_call | solution.py:390
  423.7 97.7 %rest.3 = bf16[1536,1280]{1,0:T(8,128)(2,1)} custom-call(bf16[3,512,1280]{2,1,0:T(8,128)(2,1)} %attn.3.att_ref, bf16[3,512,1280]{2,1,0:T(8,128)(2,1)} %bitcast.44, bf16[2,2,1280,1280]{3,2,1,0:T(8,128)(2,1)} %bitcast.47, f32[2,2,1280]{2,1,0:T(2,128)} %ab_ref.3, f32[2,3,2,1280]{3,2,1,0:T(2,128)} %ln_ref.7, bf16[2,1280,1280]{2,1,0:T(8,128)(2,1)} %bitcast.51, ...), custom_call_target="tpu_custom_call" | custom-call | flops 75497472000 | bytes 49152000 | tf_op jit(solution)/shard_map/rest/pallas_call | solution.py:493
  521.4 11.1 %leave.1 = (bf16[3,512,1280]{2,1,0:T(8,128)(2,1)}, f32[8,1280]{1,0:T(8,128)}, bf16[3,128,1280]{2,1,0:T(8,128)(2,1)}) custom-call(s32[1]{0:T(128)} %bitcast.1.core_ref, bf16[3,512,1280]{2,1,0:T(8,128)(2,1)} %bitcast.52, bf16[2,1280,1280]{2,1,0:T(8,128)(2,1)} %w_ref.1, f32[2,1280]{1,0:T(2,128)} %pb_ref.3, bf16[3,512,1280]{2,1,0:T(8,128)(2,1)} %get-tuple-element.73.h_ref), custom_call_target="tpu_custom_call" | custom-call | flops 5033164800 | bytes 3276800 | tf_op jit(solution)/shard_map/leave/pallas_call | solution.py:522
  536.2 56.4 %conv.10 = (bf16[3,512,1280]{2,1,0:T(8,128)(2,1)}, f32[8,1280]{1,0:T(8,128)}, bf16[3,128,1280]{2,1,0:T(8,128)(2,1)}) custom-call(s32[1]{0:T(128)} %bitcast.where_ref.core_ref, bf16[3,512,1280]{2,1,0:T(8,128)(2,1)} %get-tuple-element.82.v_ref.rest_1_, bf16[3,128,1280]{2,1,0:T(8,128)(2,1)} %copy-done.14, f32[8,1280]{1,0:T(8,128)} %get-tuple-element.84.own_ref, ...), custom_call_target="tpu_custom_call" | custom-call | flops 45298483200 | bytes 29491200 | tf_op jit(solution)/shard_map/conv/pallas_call | solution.py:234
  596.3 21.5 %conv.12 = (bf16[1,256,1280]{2,1,0:T(8,128)(2,1)}, bf16[1,256,1280]{2,1,0:T(8,128)(2,1)}) custom-call(s32[1]{0:T(128)} %bitcast.where_ref.core_ref, bf16[3,512,1280]{2,1,0:T(8,128)(2,1)} %get-tuple-element.86.v_ref, bf16[3,128,1280]{2,1,0:T(8,128)(2,1)} %copy-done.2, f32[8,1280]{1,0:T(8,128)} %get-tuple-element.88.own_ref, f32[8,1280]{1,0:T(8,128)} %copy-done.8, ...), custom_call_target="tpu_custom_call" | custom-call | flops 15099494400 | bytes 29491200 | tf_op jit(solution)/shard_map/conv/pallas_call | solution.py:234
  621.2 21.2 %conv.11 = (bf16[1,256,1280]{2,1,0:T(8,128)(2,1)}, bf16[1,256,1280]{2,1,0:T(8,128)(2,1)}) custom-call(s32[1]{0:T(128)} %bitcast.where_ref.core_ref, bf16[3,512,1280]{2,1,0:T(8,128)(2,1)} %get-tuple-element.86.v_ref, bf16[3,128,1280]{2,1,0:T(8,128)(2,1)} %copy-done.2, f32[8,1280]{1,0:T(8,128)} %get-tuple-element.88.own_ref, f32[8,1280]{1,0:T(8,128)} %copy-done.8, ...), custom_call_target="tpu_custom_call" | custom-call | flops 15099494400 | bytes 29491200 | tf_op jit(solution)/shard_map/conv/pallas_call | solution.py:234
  645.0 21.2 %conv.13 = (bf16[1,256,1280]{2,1,0:T(8,128)(2,1)}, bf16[1,256,1280]{2,1,0:T(8,128)(2,1)}) custom-call(s32[1]{0:T(128)} %bitcast.where_ref.core_ref, bf16[3,512,1280]{2,1,0:T(8,128)(2,1)} %get-tuple-element.86.v_ref, bf16[3,128,1280]{2,1,0:T(8,128)(2,1)} %copy-done.2, f32[8,1280]{1,0:T(8,128)} %get-tuple-element.88.own_ref, f32[8,1280]{1,0:T(8,128)} %copy-done.8, ...), custom_call_target="tpu_custom_call" | custom-call | flops 15099494400 | bytes 29491200 | tf_op jit(solution)/shard_map/conv/pallas_call | solution.py:234
  669.9 15.5 %collective-permute-done.24 = bf16[1,256,1280]{2,1,0:T(8,128)(2,1)S(1)} collective-permute-done((bf16[1,256,1280]{2,1,0:T(8,128)(2,1)}, bf16[1,256,1280]{2,1,0:T(8,128)(2,1)S(1)}, u32[]{:S(2)}, u32[]{:S(2)}) %collective-permute-start.24) | collective-permute-done | bytes 655392 | tf_op jit(solution)/shard_map/ppermute | solution.py:589
  (90 shorter events, 36.2 us)
Async XLA Ops:
  0.0 7.1 %copy-start = (bf16[6,77,1024]{2,1,0:T(8,128)(2,1)S(1)}, bf16[6,77,1024]{2,1,0:T(8,128)(2,1)}, u32[]{:S(2)}) copy-start(bf16[6,77,1024]{2,1,0:T(8,128)(2,1)} %param.23) | copy-start | bytes 2838532
  0.0 8.1 %copy-start.18 = (bf16[6,1280]{1,0:T(8,128)(2,1)S(1)}, bf16[6,1280]{1,0:T(8,128)(2,1)}, u32[]{:S(2)}) copy-start(bf16[6,1280]{1,0:T(8,128)(2,1)} %param.22) | copy-start | bytes 46084
  2.3 20.9 %collective-permute-start.2 = (bf16[1,256,1280]{2,1,0:T(8,128)(2,1)}, bf16[1,256,1280]{2,1,0:T(8,128)(2,1)S(1)}, u32[]{:S(2)}, u32[]{:S(2)}) collective-permute-start(bf16[1,256,1280]{2,1,0:T(8,128)(2,1)} %get-tuple-element.98), channel_id=1, source_target_pairs={{0,2},{1,0},{2,3},{3,1},{4,6},{5,4},{6,7},{7,5},{8,10},{9,8},{10,1... | collective-permute-start | bytes 1966088 | tf_op jit(solution)/shard_map/ppermute | solution.py:549
  5.5 17.7 %collective-permute-start.3 = (bf16[1,256,1280]{2,1,0:T(8,128)(2,1)S(1)}, bf16[1,256,1280]{2,1,0:T(8,128)(2,1)S(1)}, u32[]{:S(2)}, u32[]{:S(2)}) collective-permute-start(bf16[1,256,1280]{2,1,0:T(8,128)(2,1)S(1)} %get-tuple-element.97), channel_id=1, source_target_pairs={{1,2},{2,1},{0,0},{3,3},{5,6},{6,5},{4,4},{7,7},{9,10},{10,9},{8,8... | collective-permute-start | bytes 1966088 | tf_op jit(solution)/shard_map/ppermute | solution.py:549
  23.2 1.1 copy-start.6
  26.7 7.3 %collective-permute-start.4 = (bf16[1,128,1280]{2,1,0:T(8,128)(2,1)}, bf16[1,128,1280]{2,1,0:T(8,128)(2,1)S(1)}, u32[]{:S(2)}, u32[]{:S(2)}) collective-permute-start(bf16[1,128,1280]{2,1,0:T(8,128)(2,1)} %get-tuple-element.55), channel_id=1, source_target_pairs={{0,1},{1,0},{2,3},{3,2},{4,5},{5,4},{6,7},{7,6},{8,9},{9,8},{10,11... | collective-permute-start | bytes 983048 | tf_op jit(solution)/shard_map/ppermute | solution.py:565
  28.0 5.9 collective-permute-start.5
  31.4 28.2 %collective-permute-start = (bf16[2,256,1280]{2,1,0:T(8,128)(2,1)}, bf16[2,256,1280]{2,1,0:T(8,128)(2,1)S(1)}, u32[]{:S(2)}, u32[]{:S(2)}) collective-permute-start(bf16[2,256,1280]{2,1,0:T(8,128)(2,1)} %get-tuple-element.100), channel_id=1, source_target_pairs={{0,2},{1,0},{2,3},{3,1},{4,6},{5,4},{6,7},{7,5},{8,10},{9,8},{10,1... | collective-permute-start | bytes 3932168 | tf_op jit(solution)/shard_map/ppermute | solution.py:549
  31.8 27.8 %collective-permute-start.1 = (bf16[2,256,1280]{2,1,0:T(8,128)(2,1)}, bf16[2,256,1280]{2,1,0:T(8,128)(2,1)S(1)}, u32[]{:S(2)}, u32[]{:S(2)}) collective-permute-start(bf16[2,256,1280]{2,1,0:T(8,128)(2,1)} %get-tuple-element.99), channel_id=1, source_target_pairs={{1,2},{2,1},{0,0},{3,3},{5,6},{6,5},{4,4},{7,7},{9,10},{10,9},{8,8... | collective-permute-start | bytes 3932168 | tf_op jit(solution)/shard_map/ppermute | solution.py:549
  59.6 1.1 copy-start.3
  59.6 1.5 copy-start.4
  64.5 4.2 collective-permute-start.6
  66.9 1.8 collective-permute-start.7
  108.7 2.7 collective-permute-start.8
  109.1 2.3 collective-permute-start.9
  169.7 1.3 collective-permute-start.10
  197.7 9.6 %collective-permute-start.12 = (bf16[3,1280,512]{2,1,0:T(8,128)(2,1)}, bf16[3,1280,512]{2,1,0:T(8,128)(2,1)}, u32[]{:S(2)}, u32[]{:S(2)}) collective-permute-start(bf16[3,1280,512]{2,1,0:T(8,128)(2,1)} %values.2.v0_ref), channel_id=1, source_target_pairs={{0,1},{1,0},{2,3},{3,2},{4,5},{5,4},{6,7},{7,6},{8,9},{9,8},{10,11... | collective-permute-start | bytes 11796488 | tf_op jit(solution)/shard_map/ppermute | solution.py:565
  198.1 12.0 %collective-permute-start.11 = (bf16[3,512,1280]{2,1,0:T(8,128)(2,1)}, bf16[3,512,1280]{2,1,0:T(8,128)(2,1)}, u32[]{:S(2)}, u32[]{:S(2)}) collective-permute-start(bf16[3,512,1280]{2,1,0:T(8,128)(2,1)} %get-tuple-element.76.k0_ref), channel_id=1, source_target_pairs={{0,1},{1,0},{2,3},{3,2},{4,5},{5,4},{6,7},{7,6},{8,9},{9,8},{10,11... | collective-permute-start | bytes 11796488 | tf_op jit(solution)/shard_map/ppermute | solution.py:565
  369.5 9.6 %collective-permute-start.14 = (bf16[3,1280,512]{2,1,0:T(8,128)(2,1)}, bf16[3,1280,512]{2,1,0:T(8,128)(2,1)}, u32[]{:S(2)}, u32[]{:S(2)}) collective-permute-start(bf16[3,1280,512]{2,1,0:T(8,128)(2,1)} %values.3.v0_ref), channel_id=1, source_target_pairs={{0,1},{1,0},{2,3},{3,2},{4,5},{5,4},{6,7},{7,6},{8,9},{9,8},{10,11... | collective-permute-start | bytes 11796488 | tf_op jit(solution)/shard_map/ppermute | solution.py:565
  369.8 12.0 %collective-permute-start.13 = (bf16[3,512,1280]{2,1,0:T(8,128)(2,1)}, bf16[3,512,1280]{2,1,0:T(8,128)(2,1)}, u32[]{:S(2)}, u32[]{:S(2)}) collective-permute-start(bf16[3,512,1280]{2,1,0:T(8,128)(2,1)} %get-tuple-element.81.k0_ref), channel_id=1, source_target_pairs={{0,1},{1,0},{2,3},{3,2},{4,5},{5,4},{6,7},{7,6},{8,9},{9,8},{10,11... | collective-permute-start | bytes 11796488 | tf_op jit(solution)/shard_map/ppermute | solution.py:565
  532.6 2.6 collective-permute-start.15
  532.9 2.3 collective-permute-start.16
  592.6 2.7 collective-permute-start.17
  593.0 2.3 collective-permute-start.18
  617.8 51.9 %collective-permute-start.21 = (bf16[1,256,1280]{2,1,0:T(8,128)(2,1)}, bf16[1,256,1280]{2,1,0:T(8,128)(2,1)S(1)}, u32[]{:S(2)}, u32[]{:S(2)}) collective-permute-start(bf16[1,256,1280]{2,1,0:T(8,128)(2,1)} %get-tuple-element.91), channel_id=1, source_target_pairs={{2,1},{1,2},{0,0},{3,3},{6,5},{5,6},{4,4},{7,7},{10,9},{9,10},{8,8... | collective-permute-start | bytes 1966088 | tf_op jit(solution)/shard_map/ppermute | solution.py:590
  619.6 50.2 %collective-permute-start.22 = (bf16[1,256,1280]{2,1,0:T(8,128)(2,1)}, bf16[1,256,1280]{2,1,0:T(8,128)(2,1)S(1)}, u32[]{:S(2)}, u32[]{:S(2)}) collective-permute-start(bf16[1,256,1280]{2,1,0:T(8,128)(2,1)} %get-tuple-element.92), channel_id=1, source_target_pairs={{2,0},{0,1},{3,2},{1,3},{6,4},{4,5},{7,6},{5,7},{10,8},{8,9},{11,1... | collective-permute-start | bytes 1966088 | tf_op jit(solution)/shard_map/ppermute | solution.py:589
  642.5 25.6 %collective-permute-start.19 = (bf16[1,256,1280]{2,1,0:T(8,128)(2,1)}, bf16[1,256,1280]{2,1,0:T(8,128)(2,1)S(1)}, u32[]{:S(2)}, u32[]{:S(2)}) collective-permute-start(bf16[1,256,1280]{2,1,0:T(8,128)(2,1)} %get-tuple-element.89), channel_id=1, source_target_pairs={{2,1},{1,2},{0,0},{3,3},{6,5},{5,6},{4,4},{7,7},{10,9},{9,10},{8,8... | collective-permute-start | bytes 1966088 | tf_op jit(solution)/shard_map/ppermute | solution.py:590
  644.2 25.3 %collective-permute-start.20 = (bf16[1,256,1280]{2,1,0:T(8,128)(2,1)}, bf16[1,256,1280]{2,1,0:T(8,128)(2,1)S(1)}, u32[]{:S(2)}, u32[]{:S(2)}) collective-permute-start(bf16[1,256,1280]{2,1,0:T(8,128)(2,1)} %get-tuple-element.90), channel_id=1, source_target_pairs={{2,0},{0,1},{3,2},{1,3},{6,4},{4,5},{7,6},{5,7},{10,8},{8,9},{11,1... | collective-permute-start | bytes 1966088 | tf_op jit(solution)/shard_map/ppermute | solution.py:589
  666.3 3.6 collective-permute-start.23
  668.0 17.4 %collective-permute-start.24 = (bf16[1,256,1280]{2,1,0:T(8,128)(2,1)}, bf16[1,256,1280]{2,1,0:T(8,128)(2,1)S(1)}, u32[]{:S(2)}, u32[]{:S(2)}) collective-permute-start(bf16[1,256,1280]{2,1,0:T(8,128)(2,1)} %get-tuple-element.94), channel_id=1, source_target_pairs={{2,0},{0,1},{3,2},{1,3},{6,4},{4,5},{7,6},{5,7},{10,8},{8,9},{11,1... | collective-permute-start | bytes 1966088 | tf_op jit(solution)/shard_map/ppermute | solution.py:589
  669.7 18.3 %copy-start.1 = (bf16[6,77,1024]{2,1,0:T(8,128)(2,1)S(1)}, bf16[6,77,1024]{2,1,0:T(8,128)(2,1)}, u32[]{:S(2)}) copy-start(bf16[6,77,1024]{2,1,0:T(8,128)(2,1)} %param.23) | copy-start | bytes 2838532
  686.1 1.9 copy-start.10
  (12 other events, 9.1 us)

commit v3 on v2

--- a/solution.py
+++ b/solution.py
@@ -545,10 +545,12 @@
     halves = flat.reshape(2, lat, rows_n * cols, chan)
     going, staying = lax.dynamic_index_in_dim(halves, 1 - core, keepdims=False), lax.dynamic_index_in_dim(halves, core, keepdims=False)
 
-    def spread(part):
-        return lax.ppermute(going[part], 'sp', pairs_of('02 10 23 31')), lax.ppermute(staying[part], 'sp', pairs_of('12 21 00 33'))
-
-    early, late = spread(slice(lat - 1, lat)), spread(slice(0, lat - 1))
+    def spread(away, here):
+        return lax.ppermute(away, 'sp', pairs_of('02 10 23 31')), lax.ppermute(here, 'sp', pairs_of('12 21 00 33'))
+
+    early = spread(going[lat - 1:], staying[lat - 1:])
+    *rest, context = lax.optimization_barrier((going[:lat - 1], staying[:lat - 1], context))
+    late = spread(*rest)
 
     temb = lax.dynamic_slice(time_emb, (chip * lat, 0), (lat, chan))
     temb = jax.nn.silu(temb.astype(F32)).astype(BF)
@@ -563,10 +565,10 @@
     conv_w = res_conv_w.reshape(-1, KERNEL, KERNEL * chan, chan)
 
     swap = lambda a: lax.ppermute(a, 'sp', SWAP)
-    early, kc, vc, tembs = lax.optimization_barrier((early, kc, vc, tembs))
+    early, kc, vc, tembs[0] = lax.optimization_barrier((early, kc, vc, tembs[0]))
     v, own, edge = gather_call(where, *early, 2)
     into = conv_call(where, v, swap(edge), own, swap(own), res_norm, res_conv_b, conv_w, 0, 0, temb=tembs[0], base=2, lat=1)
-    late, v, into = lax.optimization_barrier((late, v, into))
+    late, v, into, tembs[1] = lax.optimization_barrier((late, v, into, tembs[1]))
     v, own, edge = gather_call(where, *late, 0, into=v)
     t, sums_t, edge = conv_call(where, v, swap(edge), own, swap(own), res_norm, res_conv_b, conv_w, 0, 0, temb=tembs[0], into=into, base=0, lat=2)
     h, sums_h, _ = conv_call(where, t, swap(edge), sums_t, swap(sums_t), res_norm, res_conv_b, conv_w, 0, 1, res=v)
@@ -584,8 +586,8 @@
     t, sums_t, edge = conv_call(where, h, swap(edge), sums_h, swap(sums_h), res_norm, res_conv_b, conv_w, 1, 0, temb=tembs[1])
     edge, peer = swap(edge), swap(sums_t)
     lows, highs = [], []
-    for l in range(lat):
-        going, staying = conv_call(where, t, edge, sums_t, peer, res_norm, res_conv_b, conv_w, 1, 1, res=h, base=l, lat=1, want_sums=False)
+    for base, some in ((0, 2), (2, 1)):
+        going, staying = conv_call(where, t, edge, sums_t, peer, res_norm, res_conv_b, conv_w, 1, 1, res=h, base=base, lat=some, want_sums=False)
         first = lax.ppermute(going, 'sp', pairs_of('20 01 32 13'))
         third = lax.ppermute(staying, 'sp', pairs_of('21 12 00 33'))
         lows.append(jnp.where(core == 0, third, first))

time: 693 us -> 687 us (level)
    ppermute x3 -> x2, waiting for transfers between devices: 15.5 us -> 20.2 us  [device_block(): first = lax.ppermute(going, 'sp', pairs_of('20 01 32 13'))]
    pallas_call x7 -> x6, Pallas kernels: 238 us -> 234 us  [conv_call(): pl.pallas_call(body, grid_spec=pltpu.PrefetchScalarGridSpec(num_scalar_pr...]
  transfers between devices with their start and end apart: 25 -> 23, of which waited for: 9 -> 8; matrix products, arithmetic and copies ran while one was open for 2% -> 2% of each run, Pallas kernels for 13% -> 10%
where the time goes in v3:
time: 687 us; the launch traced here: 683 us
  Pallas kernels  603 us (88%)
  waiting for transfers between devices  34.7 us (5%)
  starting transfers between devices  19.5 us (3%)
  local copies, waits for them, and re-layouts  14.6 us (2%)
    pallas_call x6, Pallas kernels, conv_call(): pl.pallas_call(body, grid_spec=pltpu.PrefetchScalarGridSpec(num_scalar_pr...  234 us
    pallas_call x2, Pallas kernels, rest_call(): pl.pallas_call(functools.partial(rest_kernel, layer=layer, ctx_len=ctx_le...  196 us
    pallas_call x2, Pallas kernels, attn_call(): pl.pallas_call(functools.partial(attn_kernel, pairs=pairs), grid=(lat, ch...  83.7 us
    pallas_call x4, Pallas kernels, linear_call(): pl.pallas_call(kernel, grid=(lat,), in_specs=[major((1, tok, chan)), fixe...  36.5 us
    ppermute x2, waiting for transfers between devices, device_block(): first = lax.ppermute(going, 'sp', pairs_of('20 01 32 13'))  20.2 us
    pallas_call x1, Pallas kernels, enter_call(): pl.pallas_call(enter_kernel, grid=(lat,), in_specs=[row, whole(own), whol...  17.1 us
    ppermute x15, waiting for transfers between devices, device_block(): swap = lambda a: lax.ppermute(a, 'sp', SWAP)  14.5 us
  transfers between devices with their start and end apart: 23, of which 8 were waited for; matrix products, arithmetic and copies ran while one was open for 2% of the time, Pallas kernels for 10%

profile of v3, /device:TPU:0, one launch (start us, length us, event | category | flops | bytes accessed | tf_op | source)
XLA Modules:
  0.0 682.7 jit_solution(15626742094304934681)
XLA Ops:
  0.0 2.3 dynamic-slice_bitcast_fusion.2
  2.3 3.2 collective-permute-start.2
  6.2 3.4 dynamic-slice_bitcast_fusion
  10.7 3.1 fusion.6.rest_0_
  13.8 8.9 %context.1 = (bf16[2,3,80,1280]{3,2,1,0:T(8,128)(2,1)}, bf16[2,3,1280,128]{3,2,1,0:T(8,128)(2,1)}) custom-call(bf16[3,128,1024]{2,1,0:T(8,128)(2,1)} %pad.4.ctx_ref, bf16[2,2,1280,1024]{3,2,1,0:T(8,128)(2,1)} %bitcast.49), custom_call_target="tpu_custom_call" | custom-call | flops 4026531840 | bytes 10485760 | tf_op jit(solution)/shard_map/context/pallas_call | solution.py:409
  23.8 2.4 gather.2
  27.6 2.1 collective-permute-start.1
  30.3 3.1 fusion.9.rest_0_
  34.1 21.2 %conv.6 = (bf16[3,512,1280]{2,1,0:T(8,128)(2,1)}, f32[8,1280]{1,0:T(8,128)}, bf16[3,128,1280]{2,1,0:T(8,128)(2,1)}) custom-call(s32[1]{0:T(128)} %bitcast.where_ref.core_ref, bf16[3,512,1280]{2,1,0:T(8,128)(2,1)} %get-tuple-element.67.v_ref.rest_4_, bf16[1,128,1280]{2,1,0:T(8,128)(2,1)} %copy-done.8, f32[8,1280]{1,0:T(8,128)} %get-tuple-element.60.own_ref, ...), custom_call_target="tpu_custom_call" | custom-call | flops 15099494400 | bytes 29491200 | tf_op jit(solution)/shard_map/conv/pallas_call | solution.py:234
  56.9 3.4 gather.3
  60.2 2.4 collective-permute-start.6
  65.3 39.1 %conv.7 = (bf16[3,512,1280]{2,1,0:T(8,128)(2,1)}, f32[8,1280]{1,0:T(8,128)}, bf16[3,128,1280]{2,1,0:T(8,128)(2,1)}) custom-call(s32[1]{0:T(128)} %bitcast.where_ref.core_ref, bf16[3,512,1280]{2,1,0:T(8,128)(2,1)} %get-tuple-element.68.v_ref.rest_1_, bf16[2,128,1280]{2,1,0:T(8,128)(2,1)} %copy-done.7, ...), custom_call_target="tpu_custom_call", output_to_operand_aliasing={{0}: (9, {}), {2}: (10, {})} | custom-call | flops 30198988800 | bytes 29491200 | tf_op jit(solution)/shard_map/conv/pallas_call | solution.py:234
  104.9 2.1 collective-permute-done.9.peer_ref
  108.1 57.2 %conv.8 = (bf16[3,512,1280]{2,1,0:T(8,128)(2,1)}, f32[8,1280]{1,0:T(8,128)}, bf16[3,128,1280]{2,1,0:T(8,128)(2,1)}) custom-call(s32[1]{0:T(128)} %bitcast.where_ref.core_ref, bf16[3,512,1280]{2,1,0:T(8,128)(2,1)} %get-tuple-element.74.v_ref, bf16[3,128,1280]{2,1,0:T(8,128)(2,1)} %copy-done.13, f32[8,1280]{1,0:T(8,128)} %get-tuple-element.76.own_ref, ...), custom_call_target="tpu_custom_call" | custom-call | flops 45298483200 | bytes 29491200 | tf_op jit(solution)/shard_map/conv/pallas_call | solution.py:234
  167.2 17.1 %enter.1 = (bf16[3,512,1280]{2,1,0:T(8,128)(2,1)}, bf16[3,512,1280]{2,1,0:T(8,128)(2,1)}, bf16[3,512,1280]{2,1,0:T(8,128)(2,1)}) custom-call(bf16[3,512,1280]{2,1,0:T(8,128)(2,1)} %get-tuple-element.77.h_ref, f32[8,1280]{1,0:T(8,128)} %get-tuple-element.78.own_ref, f32[8,1280]{1,0:T(8,128)} %copy-done.17, f32[2,1280]{1,0:T(2,128)} %norm_ref.10, ...), custom_call_target="tpu_custom_call" | custom-call | flops 10066329600 | bytes 6553600 | tf_op jit(solution)/shard_map/enter/pallas_call | solution.py:311
  184.3 9.1 %values.2.v0_ref = bf16[3,1280,512]{2,1,0:T(8,128)(2,1)} custom-call(bf16[3,512,1280]{2,1,0:T(8,128)(2,1)} %get-tuple-element.79.n_ref, bf16[2,3,1280,1280]{3,2,1,0:T(8,128)(2,1)} %bitcast.36), custom_call_target="tpu_custom_call" | custom-call | flops 209715200 | bytes 3276800 | tf_op jit(solution)/shard_map/values/pallas_call | solution.py:348
  193.9 9.1 %queries.2.q_ref = bf16[3,512,1280]{2,1,0:T(8,128)(2,1)} custom-call(bf16[3,512,1280]{2,1,0:T(8,128)(2,1)} %get-tuple-element.79.n_ref, bf16[2,3,1280,1280]{3,2,1,0:T(8,128)(2,1)} %bitcast.37), custom_call_target="tpu_custom_call" | custom-call | flops 209715200 | bytes 3276800 | tf_op jit(solution)/shard_map/queries/pallas_call | solution.py:348
  203.0 2.7 collective-permute-done.11.k1_ref
  205.8 41.9 %attn.2.att_ref = bf16[3,512,1280]{2,1,0:T(8,128)(2,1)} custom-call(bf16[3,512,1280]{2,1,0:T(8,128)(2,1)} %queries.2.q_ref, bf16[3,512,1280]{2,1,0:T(8,128)(2,1)} %get-tuple-element.80.k0_ref, bf16[3,512,1280]{2,1,0:T(8,128)(2,1)} %collective-permute-done.11.k1_ref, bf16[3,1280,512]{2,1,0:T(8,128)(2,1)} %values.2.v0_ref, ...), custom_call_target="tpu_custom_call" | custom-call | flops 8053063680 | bytes 23592960 | tf_op jit(solution)/shard_map/attn/pallas_call | solution.py:390
  247.7 98.0 %rest.2 = bf16[1536,1280]{1,0:T(8,128)(2,1)} custom-call(bf16[3,512,1280]{2,1,0:T(8,128)(2,1)} %attn.2.att_ref, bf16[3,512,1280]{2,1,0:T(8,128)(2,1)} %get-tuple-element.81.u_ref, bf16[2,2,1280,1280]{3,2,1,0:T(8,128)(2,1)} %bitcast.45, f32[2,2,1280]{2,1,0:T(2,128)} %ab_ref.3, f32[2,3,2,1280]{3,2,1,0:T(2,128)} %ln_ref.7, bf16[2,1280,1280]{2,1,0:T(8,128)(2,1)} %bitcast.50, ...), custom_call_target="tpu_custom_call" | custom-call | flops 75497472000 | bytes 49152000 | tf_op jit(solution)/shard_map/rest/pallas_call | solution.py:493
  345.7 10.3 %keys.1 = (bf16[3,512,1280]{2,1,0:T(8,128)(2,1)}, bf16[3,512,1280]{2,1,0:T(8,128)(2,1)}) custom-call(bf16[3,512,1280]{2,1,0:T(8,128)(2,1)} %bitcast.43, f32[2,3,2,1280]{3,2,1,0:T(2,128)} %ln_ref.7, bf16[2,3,1280,1280]{3,2,1,0:T(8,128)(2,1)} %bitcast.38), custom_call_target="tpu_custom_call" | custom-call | flops 5033164800 | bytes 3276800 | tf_op jit(solution)/shard_map/keys/pallas_call | solution.py:331
  356.0 9.1 %values.3.v0_ref = bf16[3,1280,512]{2,1,0:T(8,128)(2,1)} custom-call(bf16[3,512,1280]{2,1,0:T(8,128)(2,1)} %get-tuple-element.84.n_ref, bf16[2,3,1280,1280]{3,2,1,0:T(8,128)(2,1)} %bitcast.39), custom_call_target="tpu_custom_call" | custom-call | flops 209715200 | bytes 3276800 | tf_op jit(solution)/shard_map/values/pallas_call | solution.py:348
  365.7 9.1 %queries.3.q_ref = bf16[3,512,1280]{2,1,0:T(8,128)(2,1)} custom-call(bf16[3,512,1280]{2,1,0:T(8,128)(2,1)} %get-tuple-element.84.n_ref, bf16[2,3,1280,1280]{3,2,1,0:T(8,128)(2,1)} %bitcast.40), custom_call_target="tpu_custom_call" | custom-call | flops 209715200 | bytes 3276800 | tf_op jit(solution)/shard_map/queries/pallas_call | solution.py:348
  374.8 2.7 collective-permute-done.13.k1_ref
  377.5 41.9 %attn.3.att_ref = bf16[3,512,1280]{2,1,0:T(8,128)(2,1)} custom-call(bf16[3,512,1280]{2,1,0:T(8,128)(2,1)} %queries.3.q_ref, bf16[3,512,1280]{2,1,0:T(8,128)(2,1)} %get-tuple-element.85.k0_ref, bf16[3,512,1280]{2,1,0:T(8,128)(2,1)} %collective-permute-done.13.k1_ref, bf16[3,1280,512]{2,1,0:T(8,128)(2,1)} %values.3.v0_ref, ...), custom_call_target="tpu_custom_call" | custom-call | flops 8053063680 | bytes 23592960 | tf_op jit(solution)/shard_map/attn/pallas_call | solution.py:390
  419.4 97.7 %rest.3 = bf16[1536,1280]{1,0:T(8,128)(2,1)} custom-call(bf16[3,512,1280]{2,1,0:T(8,128)(2,1)} %attn.3.att_ref, bf16[3,512,1280]{2,1,0:T(8,128)(2,1)} %bitcast.44, bf16[2,2,1280,1280]{3,2,1,0:T(8,128)(2,1)} %bitcast.47, f32[2,2,1280]{2,1,0:T(2,128)} %ab_ref.3, f32[2,3,2,1280]{3,2,1,0:T(2,128)} %ln_ref.7, bf16[2,1280,1280]{2,1,0:T(8,128)(2,1)} %bitcast.51, ...), custom_call_target="tpu_custom_call" | custom-call | flops 75497472000 | bytes 49152000 | tf_op jit(solution)/shard_map/rest/pallas_call | solution.py:493
  517.0 11.1 %leave.1 = (bf16[3,512,1280]{2,1,0:T(8,128)(2,1)}, f32[8,1280]{1,0:T(8,128)}, bf16[3,128,1280]{2,1,0:T(8,128)(2,1)}) custom-call(s32[1]{0:T(128)} %bitcast.1.core_ref, bf16[3,512,1280]{2,1,0:T(8,128)(2,1)} %bitcast.52, bf16[2,1280,1280]{2,1,0:T(8,128)(2,1)} %w_ref.1, f32[2,1280]{1,0:T(2,128)} %pb_ref.3, bf16[3,512,1280]{2,1,0:T(8,128)(2,1)} %get-tuple-element.77.h_ref), custom_call_target="tpu_custom_call" | custom-call | flops 5033164800 | bytes 3276800 | tf_op jit(solution)/shard_map/leave/pallas_call | solution.py:522
  531.8 56.5 %conv.9 = (bf16[3,512,1280]{2,1,0:T(8,128)(2,1)}, f32[8,1280]{1,0:T(8,128)}, bf16[3,128,1280]{2,1,0:T(8,128)(2,1)}) custom-call(s32[1]{0:T(128)} %bitcast.where_ref.core_ref, bf16[3,512,1280]{2,1,0:T(8,128)(2,1)} %get-tuple-element.86.v_ref.rest_1_, bf16[3,128,1280]{2,1,0:T(8,128)(2,1)} %copy-done.14, f32[8,1280]{1,0:T(8,128)} %get-tuple-element.88.own_ref, ...), custom_call_target="tpu_custom_call" | custom-call | flops 45298483200 | bytes 29491200 | tf_op jit(solution)/shard_map/conv/pallas_call | solution.py:234
  592.0 39.0 %conv.10 = (bf16[2,256,1280]{2,1,0:T(8,128)(2,1)}, bf16[2,256,1280]{2,1,0:T(8,128)(2,1)}) custom-call(s32[1]{0:T(128)} %bitcast.where_ref.core_ref, bf16[3,512,1280]{2,1,0:T(8,128)(2,1)} %get-tuple-element.90.v_ref, bf16[3,128,1280]{2,1,0:T(8,128)(2,1)} %copy-done.4, f32[8,1280]{1,0:T(8,128)} %get-tuple-element.92.own_ref, f32[8,1280]{1,0:T(8,128)} %copy-done.9, ...), custom_call_target="tpu_custom_call" | custom-call | flops 30198988800 | bytes 29491200 | tf_op jit(solution)/shard_map/conv/pallas_call | solution.py:234
  634.5 21.3 %conv.11 = (bf16[1,256,1280]{2,1,0:T(8,128)(2,1)}, bf16[1,256,1280]{2,1,0:T(8,128)(2,1)}) custom-call(s32[1]{0:T(128)} %bitcast.where_ref.core_ref, bf16[3,512,1280]{2,1,0:T(8,128)(2,1)} %get-tuple-element.90.v_ref, bf16[3,128,1280]{2,1,0:T(8,128)(2,1)} %copy-done.4, f32[8,1280]{1,0:T(8,128)} %get-tuple-element.92.own_ref, f32[8,1280]{1,0:T(8,128)} %copy-done.9, ...), custom_call_target="tpu_custom_call" | custom-call | flops 15099494400 | bytes 29491200 | tf_op jit(solution)/shard_map/conv/pallas_call | solution.py:234
  658.3 20.2 %collective-permute-done.22 = bf16[1,256,1280]{2,1,0:T(8,128)(2,1)S(1)} collective-permute-done((bf16[1,256,1280]{2,1,0:T(8,128)(2,1)}, bf16[1,256,1280]{2,1,0:T(8,128)(2,1)S(1)}, u32[]{:S(2)}, u32[]{:S(2)}) %collective-permute-start.22) | collective-permute-done | bytes 655392 | tf_op jit(solution)/shard_map/ppermute | solution.py:591
  680.1 2.2 pad_maximum_fusion
  (82 shorter events, 29.1 us)
Async XLA Ops:
  0.0 9.7 %copy-start = (bf16[6,77,1024]{2,1,0:T(8,128)(2,1)S(1)}, bf16[6,77,1024]{2,1,0:T(8,128)(2,1)}, u32[]{:S(2)}) copy-start(bf16[6,77,1024]{2,1,0:T(8,128)(2,1)} %param.23) | copy-start | bytes 2838532
  0.0 9.6 %copy-start.12 = (f32[2,1280]{1,0:T(2,128)S(1)}, f32[2,1280]{1,0:T(2,128)}, u32[]{:S(2)}) copy-start(f32[2,1280]{1,0:T(2,128)} %param.28) | copy-start | bytes 30724
  2.3 8.4 %copy-start.18 = (bf16[6,1280]{1,0:T(8,128)(2,1)S(1)}, bf16[6,1280]{1,0:T(8,128)(2,1)}, u32[]{:S(2)}) copy-start(bf16[6,1280]{1,0:T(8,128)(2,1)} %param.22) | copy-start | bytes 46084
  2.3 20.4 %collective-permute-start.2 = (bf16[1,256,1280]{2,1,0:T(8,128)(2,1)}, bf16[1,256,1280]{2,1,0:T(8,128)(2,1)S(1)}, u32[]{:S(2)}, u32[]{:S(2)}) collective-permute-start(bf16[1,256,1280]{2,1,0:T(8,128)(2,1)} %get-tuple-element.100), channel_id=1, source_target_pairs={{0,2},{1,0},{2,3},{3,1},{4,6},{5,4},{6,7},{7,5},{8,10},{9,8},{10,1... | collective-permute-start | bytes 1966088 | tf_op jit(solution)/shard_map/ppermute | solution.py:549
  5.6 17.2 %collective-permute-start.3 = (bf16[1,256,1280]{2,1,0:T(8,128)(2,1)S(1)}, bf16[1,256,1280]{2,1,0:T(8,128)(2,1)S(1)}, u32[]{:S(2)}, u32[]{:S(2)}) collective-permute-start(bf16[1,256,1280]{2,1,0:T(8,128)(2,1)S(1)} %get-tuple-element.99), channel_id=1, source_target_pairs={{1,2},{2,1},{0,0},{3,3},{5,6},{6,5},{4,4},{7,7},{9,10},{10,9},{8,8... | collective-permute-start | bytes 1966088 | tf_op jit(solution)/shard_map/ppermute | solution.py:549
  22.7 1.1 copy-start.6
  26.2 7.2 %collective-permute-start.4 = (bf16[1,128,1280]{2,1,0:T(8,128)(2,1)}, bf16[1,128,1280]{2,1,0:T(8,128)(2,1)S(1)}, u32[]{:S(2)}, u32[]{:S(2)}) collective-permute-start(bf16[1,128,1280]{2,1,0:T(8,128)(2,1)} %get-tuple-element.59), channel_id=1, source_target_pairs={{0,1},{1,0},{2,3},{3,2},{4,5},{5,4},{6,7},{7,6},{8,9},{9,8},{10,11... | collective-permute-start | bytes 983048 | tf_op jit(solution)/shard_map/ppermute | solution.py:567
  27.6 27.7 %collective-permute-start = (bf16[2,256,1280]{2,1,0:T(8,128)(2,1)}, bf16[2,256,1280]{2,1,0:T(8,128)(2,1)S(1)}, u32[]{:S(2)}, u32[]{:S(2)}) collective-permute-start(bf16[2,256,1280]{2,1,0:T(8,128)(2,1)} %get-tuple-element.51), channel_id=1, source_target_pairs={{0,2},{1,0},{2,3},{3,1},{4,6},{5,4},{6,7},{7,5},{8,10},{9,8},{10,1... | collective-permute-start | bytes 3932168 | tf_op jit(solution)/shard_map/ppermute | solution.py:549
  27.6 27.8 %collective-permute-start.1 = (bf16[2,256,1280]{2,1,0:T(8,128)(2,1)}, bf16[2,256,1280]{2,1,0:T(8,128)(2,1)S(1)}, u32[]{:S(2)}, u32[]{:S(2)}) collective-permute-start(bf16[2,256,1280]{2,1,0:T(8,128)(2,1)} %get-tuple-element.52), channel_id=1, source_target_pairs={{1,2},{2,1},{0,0},{3,3},{5,6},{6,5},{4,4},{7,7},{9,10},{10,9},{8,8... | collective-permute-start | bytes 3932168 | tf_op jit(solution)/shard_map/ppermute | solution.py:549
  29.8 3.6 collective-permute-start.5
  55.4 1.1 copy-start.2
  55.4 1.5 copy-start.3
  60.2 4.1 collective-permute-start.6
  62.6 1.8 collective-permute-start.7
  104.4 2.7 collective-permute-start.8
  104.8 2.3 collective-permute-start.9
  107.0 1.0 copy-start.13
  165.3 1.3 collective-permute-start.10
  193.4 9.6 %collective-permute-start.12 = (bf16[3,1280,512]{2,1,0:T(8,128)(2,1)}, bf16[3,1280,512]{2,1,0:T(8,128)(2,1)}, u32[]{:S(2)}, u32[]{:S(2)}) collective-permute-start(bf16[3,1280,512]{2,1,0:T(8,128)(2,1)} %values.2.v0_ref), channel_id=1, source_target_pairs={{0,1},{1,0},{2,3},{3,2},{4,5},{5,4},{6,7},{7,6},{8,9},{9,8},{10,11... | collective-permute-start | bytes 11796488 | tf_op jit(solution)/shard_map/ppermute | solution.py:567
  193.7 12.0 %collective-permute-start.11 = (bf16[3,512,1280]{2,1,0:T(8,128)(2,1)}, bf16[3,512,1280]{2,1,0:T(8,128)(2,1)}, u32[]{:S(2)}, u32[]{:S(2)}) collective-permute-start(bf16[3,512,1280]{2,1,0:T(8,128)(2,1)} %get-tuple-element.80.k0_ref), channel_id=1, source_target_pairs={{0,1},{1,0},{2,3},{3,2},{4,5},{5,4},{6,7},{7,6},{8,9},{9,8},{10,11... | collective-permute-start | bytes 11796488 | tf_op jit(solution)/shard_map/ppermute | solution.py:567
  365.2 9.6 %collective-permute-start.14 = (bf16[3,1280,512]{2,1,0:T(8,128)(2,1)}, bf16[3,1280,512]{2,1,0:T(8,128)(2,1)}, u32[]{:S(2)}, u32[]{:S(2)}) collective-permute-start(bf16[3,1280,512]{2,1,0:T(8,128)(2,1)} %values.3.v0_ref), channel_id=1, source_target_pairs={{0,1},{1,0},{2,3},{3,2},{4,5},{5,4},{6,7},{7,6},{8,9},{9,8},{10,11... | collective-permute-start | bytes 11796488 | tf_op jit(solution)/shard_map/ppermute | solution.py:567
  365.5 12.0 %collective-permute-start.13 = (bf16[3,512,1280]{2,1,0:T(8,128)(2,1)}, bf16[3,512,1280]{2,1,0:T(8,128)(2,1)}, u32[]{:S(2)}, u32[]{:S(2)}) collective-permute-start(bf16[3,512,1280]{2,1,0:T(8,128)(2,1)} %get-tuple-element.85.k0_ref), channel_id=1, source_target_pairs={{0,1},{1,0},{2,3},{3,2},{4,5},{5,4},{6,7},{7,6},{8,9},{9,8},{10,11... | collective-permute-start | bytes 11796488 | tf_op jit(solution)/shard_map/ppermute | solution.py:567
  528.2 2.6 collective-permute-start.15
  528.5 2.3 collective-permute-start.16
  588.2 2.7 collective-permute-start.17
  588.6 2.3 collective-permute-start.18
  590.9 1.0 copy-start.4
  630.9 47.6 %collective-permute-start.19 = (bf16[2,256,1280]{2,1,0:T(8,128)(2,1)}, bf16[2,256,1280]{2,1,0:T(8,128)(2,1)S(1)}, u32[]{:S(2)}, u32[]{:S(2)}) collective-permute-start(bf16[2,256,1280]{2,1,0:T(8,128)(2,1)} %get-tuple-element.93), channel_id=1, source_target_pairs={{2,1},{1,2},{0,0},{3,3},{6,5},{5,6},{4,4},{7,7},{10,9},{9,10},{8,8... | collective-permute-start | bytes 3932168 | tf_op jit(solution)/shard_map/ppermute | solution.py:592
  632.9 45.7 %collective-permute-start.20 = (bf16[2,256,1280]{2,1,0:T(8,128)(2,1)}, bf16[2,256,1280]{2,1,0:T(8,128)(2,1)}, u32[]{:S(2)}, u32[]{:S(2)}) collective-permute-start(bf16[2,256,1280]{2,1,0:T(8,128)(2,1)} %get-tuple-element.94), channel_id=1, source_target_pairs={{2,0},{0,1},{3,2},{1,3},{6,4},{4,5},{7,6},{5,7},{10,8},{8,9},{11,1... | collective-permute-start | bytes 3932168 | tf_op jit(solution)/shard_map/ppermute | solution.py:591
  655.7 2.5 collective-permute-start.21
  657.5 21.0 %collective-permute-start.22 = (bf16[1,256,1280]{2,1,0:T(8,128)(2,1)}, bf16[1,256,1280]{2,1,0:T(8,128)(2,1)S(1)}, u32[]{:S(2)}, u32[]{:S(2)}) collective-permute-start(bf16[1,256,1280]{2,1,0:T(8,128)(2,1)} %get-tuple-element.96), channel_id=1, source_target_pairs={{2,0},{0,1},{3,2},{1,3},{6,4},{4,5},{7,6},{5,7},{10,8},{8,9},{11,1... | collective-permute-start | bytes 1966088 | tf_op jit(solution)/shard_map/ppermute | solution.py:591
  680.1 2.2 copy-start.1
  (10 other events, 7.1 us)
